TPU v7x, 128 devices: a whole 4x4x4 slice. The times are simulated.
128 devices in a mesh: dom: 8 (over y, x_hi), band: 8 (over z, core), sub: 2 (over x_lo).
Axes of the slice: x: 4 (x_hi: 2, x_lo: 2; x = x_hi * 2 + x_lo), y: 4, z: 4, core: 2. Of those that a mesh axis runs over, the one named last changes fastest.
Arguments:
- orbitals: float32 [8, 64, 64, 4096], P('dom', 'band', 'sub'), may hold values from -6 to 6
- occupations: float32 [8, 64], P('dom', 'band'), may hold values from 0.0003 to 0.003
- ext_potential: float32 [8, 64, 4096], P('dom', 'sub'), may hold values from 0 to 4
- core_range: int32 [8, 2], P('dom'), may hold values from 0 to 16, as said below
Outputs:
- orbitals_out: float32 [8, 64, 64, 4096], P('dom', 'band', 'sub')
- domain_potential: float32 [8, 64, 4096], P('dom', 'sub')
Inputs may be any that keep to these rules, and one draw needn't show every extreme that they name: core_range[d, 0] is 0 or 1 and core_range[d, 1] is 15 or 16.
All inputs are finite; a program needn't handle non-finite values.
Results may differ from a plain program's by a relative error of at most 0.00025.
Values sent between devices are 32-bit elements; how exact they have to be, the bound alone decides.
A program may use at most 128 MiB of HBM per device.

v0:
```python
import jax
import jax.numpy as jnp
from jax import lax
from jax.sharding import PartitionSpec as P

EDGE = 64
MARGIN = 8
BLOCK = 4
STEPS = 3


time_step = 0.2
screen = 0.02
eps = 1e-06
highest = lax.Precision.HIGHEST


def in_blocks(value, dim, length):
    dims = value.shape
    blocks = value.reshape(*dims[:dim], length, dims[dim] // length, *dims[dim + 1 :])
    return jnp.moveaxis(blocks, dim, 0)


def summed_on_arrival(value, axis, dim):
    blocks = in_blocks(value, dim, lax.axis_size(axis))
    arrived = lax.all_to_all(blocks, axis, split_axis=0, concat_axis=0, tiled=True)
    return arrived.sum(axis=0)


def with_halo(cells, sides, width):
    for axis, dim in sides:
        count = lax.axis_size(axis)
        head = lax.slice_in_dim(cells, 0, width, axis=dim)
        tail = lax.slice_in_dim(cells, cells.shape[dim] - width, cells.shape[dim], axis=dim)
        cells = jnp.concatenate(
            [
                lax.ppermute(tail, axis, [(i, (i + 1) % count) for i in range(count)]),
                cells,
                lax.ppermute(head, axis, [((i + 1) % count, i) for i in range(count)]),
            ],
            axis=dim,
        )
    return cells


def laid_out(blocks, dim):
    dims = list(blocks.shape[1:])
    dims[dim] *= blocks.shape[0]
    return jnp.moveaxis(blocks, 0, dim).reshape(dims)


def sent_to_all(value, axis):
    length = lax.axis_size(axis)
    return lax.all_to_all(
        jnp.broadcast_to(value[None], (length, *value.shape)), axis, 0, 0, tiled=True
    )


def collect(value, axis, dim):
    return laid_out(sent_to_all(value, axis), dim)


def taken_together(value, axis):
    return sent_to_all(value, axis).sum(axis=0)


def cas_table(row_ids, col_ids, length):
    product = row_ids[:, None] * col_ids[None, :] % length
    angle = 2.0 * jnp.pi / length * product.astype(jnp.float32)
    return jnp.cos(angle) + jnp.sin(angle)


def eigen_values(wave_ids, length):
    return 2.0 - 2.0 * jnp.cos(2.0 * jnp.pi / length * wave_ids.astype(jnp.float32))


def laplace(orbitals, padded_z):
    plane = EDGE * EDGE
    along_z = padded_z[:, :, 2:] + padded_z[:, :, :-2]
    column = jnp.arange(plane, dtype=jnp.int32) % EDGE
    next_y = jnp.where(
        column == EDGE - 1, jnp.roll(orbitals, EDGE - 1, 3), jnp.roll(orbitals, -1, 3)
    )
    prior_y = jnp.where(column == 0, jnp.roll(orbitals, 1 - EDGE, 3), jnp.roll(orbitals, 1, 3))
    padded_x = jnp.pad(orbitals, ((0, 0), (0, 0), (0, 0), (EDGE, EDGE)))
    along_x = padded_x[:, :, :, 2 * EDGE :] + padded_x[:, :, :, : -2 * EDGE]
    return along_z + along_x + next_y + prior_y - 6.0 * orbitals


def body(orbitals, occupations, ext_potential, core_range):
    band_count = lax.axis_size("band")
    sub_count = lax.axis_size("sub")
    dom_count = lax.axis_size("dom")
    half_z = orbitals.shape[2]
    depth_rows = half_z // band_count
    core_cells = EDGE - 2 * MARGIN
    length_x = core_cells * dom_count
    band_index = lax.axis_index("band")
    sub_index = lax.axis_index("sub")
    dom_index = lax.axis_index("dom")
    cell_ids = jnp.arange(EDGE, dtype=jnp.int32)
    all_length = jnp.arange(length_x, dtype=jnp.int32)
    width_kernel = cas_table(cell_ids, cell_ids, EDGE)
    core_mask = (
        (cell_ids >= core_range[0, 0] * BLOCK) & (cell_ids < core_range[0, 1] * BLOCK)
    ).astype(jnp.float32)
    plane_mask = jnp.repeat(core_mask, EDGE)
    cell_count = float(EDGE**3)
    potential = jnp.zeros_like(ext_potential[0])
    for repeat in range(STEPS):
        partial_value = jnp.einsum(
            "o,ozp->zp", occupations[0], orbitals[0] * orbitals[0], precision=highest
        )
        partial_value = partial_value * plane_mask[None, :]
        density = summed_on_arrival(partial_value, "band", 0)
        density = density.reshape(depth_rows, EDGE, EDGE)
        padded = with_halo(density, (("dom", 1),), MARGIN)
        density_grid = (
            padded[:, 2 * MARGIN : 2 * MARGIN + core_cells]
            + jnp.pad(padded[:, :MARGIN], ((0, 0), (0, core_cells - MARGIN), (0, 0)))
            + jnp.pad(padded[:, MARGIN + EDGE :], ((0, 0), (core_cells - MARGIN, 0), (0, 0)))
        )
        spectrum_y = jnp.dot(density_grid, width_kernel, precision=highest)
        pencil_cols = EDGE // (band_count * sub_count)
        depth_rank = band_index * sub_count + sub_index
        device = cell_ids // depth_rows
        depth_kernel = cas_table(
            device % sub_count * half_z + device // sub_count * depth_rows + cell_ids % depth_rows,
            cell_ids,
            EDGE,
        )
        length_kernel = cas_table(all_length, all_length, length_x)
        columns = lax.all_to_all(
            spectrum_y, ("band", "sub"), split_axis=2, concat_axis=0, tiled=True
        )
        columns = jnp.einsum("rk,rxy->kxy", depth_kernel, columns, precision=highest)
        lengthwise = lax.all_to_all(columns, "dom", split_axis=0, concat_axis=1, tiled=True)
        lengthwise = jnp.einsum("zry,rk->zky", lengthwise, length_kernel, precision=highest)
        wave_depth = dom_index * (EDGE // dom_count) + jnp.arange(
            EDGE // dom_count, dtype=jnp.int32
        )
        wave_width = depth_rank * pencil_cols + jnp.arange(pencil_cols, dtype=jnp.int32)
        green = 1.0 / (
            eigen_values(wave_depth, EDGE)[:, None, None]
            + eigen_values(all_length, length_x)[None, :, None]
            + eigen_values(wave_width, EDGE)[None, None, :]
            + screen
        )
        lengthwise = jnp.einsum("zry,rk->zky", lengthwise * green, length_kernel, precision=highest)
        columns = lax.all_to_all(lengthwise, "dom", split_axis=1, concat_axis=0, tiled=True)
        columns = jnp.einsum("rk,kxy->rxy", depth_kernel, columns, precision=highest)
        planes = lax.all_to_all(columns, ("band", "sub"), split_axis=0, concat_axis=2, tiled=True)
        local_potential = jnp.dot(planes, width_kernel, precision=highest) / (
            length_x * EDGE * EDGE
        )
        rimmed = with_halo(local_potential, (("dom", 1),), MARGIN)
        window = collect(rimmed, "band", 0)
        potential = window.reshape(half_z, EDGE * EDGE)
        half_step = jnp.exp(-0.5 * time_step * (potential + ext_potential[0]))[None, None]
        scaled = orbitals * half_step
        padded_z = with_halo(scaled, (("sub", 2),), 1)
        stepped = (scaled + 0.5 * time_step * laplace(scaled, padded_z)) * half_step
        squares = taken_together(jnp.sum(stepped * stepped, axis=(2, 3)), "sub")
        orbitals = stepped / jnp.sqrt(squares / cell_count + eps)[:, :, None, None]
    return (orbitals, potential[None])


def solution(mesh):
    return jax.shard_map(
        body,
        mesh=mesh,
        in_specs=(
            P("dom", "band", "sub", None),
            P("dom", "band"),
            P("dom", "sub", None),
            P("dom", None),
        ),
        out_specs=(P("dom", "band", "sub", None), P("dom", "sub", None)),
        check_vma=False,
    )
```

profile of v0, /device:TPU:1, one launch (start us, length us, event | category | flops | bytes accessed | tf_op | source)
XLA Modules:
  0.0 456.5 jit_solution(8184040486112104189)
XLA Ops:
  3.4 2.5 multiply_bitcast_fusion
  5.9 5.4 %fusion.28 = f32[1,32,4096]{2,0,1:T(1,128)S(1)} fusion(f32[8,32,4096]{2,1,0:T(8,128)S(1)} %multiply_bitcast_fusion, f32[1,8]{1,0:T(1,128)S(1)} %copy-done), kind=kOutput, calls=%fused_computation.40 | convolution fusion | flops 12582912 | bytes 4718624 | tf_op jit(solution)/shard_map/o,ozp->zp/dot_general | solution.py:111
  12.6 6.8 %all-to-all-start = ((f32[8,4,4096]{2,1,0:T(4,128)}), f32[8,4,4096]{2,1,0:T(4,128)S(1)}, u32[]{:S(2)}, u32[]{:S(2)}) async-start(f32[8,4,4096]{2,1,0:T(4,128)} %reshape.546), calls=%async_computation | async-start | bytes 1048576 | tf_op jit(solution)/shard_map/all_to_all | solution.py:26
  19.4 9.3 %all-to-all-done = f32[8,4,4096]{2,1,0:T(4,128)S(1)} async-done(((f32[8,4,4096]{2,1,0:T(4,128)}), f32[8,4,4096]{2,1,0:T(4,128)S(1)}, u32[]{:S(2)}, u32[]{:S(2)}) %all-to-all-start) | async-done | bytes 524320 | tf_op jit(solution)/shard_map/all_to_all | solution.py:26
  28.9 2.8 collective-permute-start
  31.7 2.5 collective-permute-start.1
  37.4 5.4 %all-to-all-start.1 = ((f32[16,1,768]{2,1,0:T(1,128)}), f32[16,1,768]{2,1,0:T(1,128)S(1)}, u32[]{:S(2)}, u32[]{:S(2)}) async-start(f32[16,1,768]{2,1,0:T(1,128)} %reshape.561), calls=%async_computation.1 | async-start | bytes 98304 | tf_op jit(solution)/shard_map/all_to_all | solution.py:133
  42.8 5.9 %all-to-all-done.1 = f32[16,1,768]{2,1,0:T(1,128)S(1)} async-done(((f32[16,1,768]{2,1,0:T(1,128)}), f32[16,1,768]{2,1,0:T(1,128)S(1)}, u32[]{:S(2)}, u32[]{:S(2)}) %all-to-all-start.1) | async-done | bytes 49184 | tf_op jit(solution)/shard_map/all_to_all | solution.py:133
  51.8 6.6 %all-to-all-start.2 = ((f32[8,1,1536]{2,1,0:T(1,128)}), f32[8,1,1536]{2,1,0:T(1,128)S(1)}, u32[]{:S(2)}, u32[]{:S(2)}) async-start(f32[8,1,1536]{2,1,0:T(1,128)} %reshape.563), calls=%async_computation.2 | async-start | bytes 98304 | tf_op jit(solution)/shard_map/all_to_all | solution.py:137
  58.5 6.6 %all-to-all-done.2 = f32[8,1,1536]{2,1,0:T(1,128)S(1)} async-done(((f32[8,1,1536]{2,1,0:T(1,128)}), f32[8,1,1536]{2,1,0:T(1,128)S(1)}, u32[]{:S(2)}, u32[]{:S(2)}) %all-to-all-start.2) | async-done | bytes 49184 | tf_op jit(solution)/shard_map/all_to_all | solution.py:137
  66.2 2.9 fusion.34
  69.1 2.9 convolution_bitcast_fusion.4
  73.1 9.0 %all_to_all.261 = f32[8,1,1536]{2,1,0:T(1,128)S(1)} all-to-all(f32[8,1,1536]{2,1,0:T(1,128)S(1)} %reshape.565), channel_id=1, replica_groups=mesh['dom'=8,'band'=8,'sub'=2] {'dom'}, dimensions={0} | all-to-all | bytes 98304 | tf_op jit(solution)/shard_map/all_to_all | solution.py:150
  84.9 11.3 %all_to_all.262 = f32[16,1,768]{2,1,0:T(1,128)S(1)} all-to-all(f32[16,1,768]{2,1,0:T(1,128)S(1)} %reshape.567), channel_id=1, replica_groups=mesh['dom'=8,'band'=8,'sub'=2] {'band','sub'}, dimensions={0} | all-to-all | bytes 98304 | tf_op jit(solution)/shard_map/all_to_all | solution.py:152
  98.3 4.7 %collective-permute-start.3 = (f32[4,8,64]{2,1,0:T(8,128)S(1)}, f32[4,8,64]{2,1,0:T(8,128)S(1)}, u32[]{:S(2)}, u32[]{:S(2)}) collective-permute-start(f32[4,8,64]{2,1,0:T(8,128)S(1)} %get-tuple-element.57), channel_id=1, source_target_pairs={{16,0},{32,16},{48,32},{64,48},{80,64},{96,80},{112,96},{0,112},{1... | collective-permute-start | bytes 24584 | tf_op jit(solution)/shard_map/ppermute | solution.py:39
  105.6 5.2 %all-to-all-start.5 = ((f32[8,1,16384]{2,1,0:T(1,128)}), f32[8,1,16384]{2,1,0:T(1,128)S(1)}, u32[]{:S(2)}, u32[]{:S(2)}) async-start(f32[8,1,16384]{2,1,0:T(1,128)} %reshape.569), calls=%async_computation.5 | async-start | bytes 1048576 | tf_op jit(solution)/shard_map/all_to_all | solution.py:54
  110.8 9.3 %all-to-all-done.5 = f32[8,1,16384]{2,1,0:T(1,128)S(1)} async-done(((f32[8,1,16384]{2,1,0:T(1,128)}), f32[8,1,16384]{2,1,0:T(1,128)S(1)}, u32[]{:S(2)}, u32[]{:S(2)}) %all-to-all-start.5) | async-done | bytes 524320 | tf_op jit(solution)/shard_map/all_to_all | solution.py:54
  120.2 2.0 reduce.10
  123.0 4.6 %copy_multiply_fusion = f32[1,8,32,4096]{3,1,2,0:T(8,128)S(1)} fusion(f32[1,8,32,4096]{3,2,1,0:T(8,128)} %param.4, f32[32,4096]{1,0:T(8,128)S(1)} %fusion.47), kind=kLoop, calls=%fused_computation.42 | loop fusion | flops 1048576 | bytes 8912896 | tf_op jit(solution)/shard_map/mul | solution.py:160
  127.8 3.7 fusion.196
  131.5 4.8 %fusion.195 = (f32[1,8,32,4033]{3,1,2,0:T(8,128)}, f32[1,8,32,4033]{3,1,2,0:T(8,128)}) fusion(f32[1,8,32,4096]{3,1,2,0:T(8,128)S(1)} %copy_multiply_fusion), kind=kLoop, calls=%fused_computation.267 | loop fusion | bytes 16519168 | tf_op jit(solution)/shard_map/jit(_roll_static)/slice | solution.py:82
  140.3 3.1 collective-permute-done.5
  143.4 10.3 %multiply_reduce_fusion.2 = (f32[8]{0:T(128)S(1)}, f32[1,8,32,4096]{3,1,2,0:T(8,128)}) fusion(f32[32,4096]{1,0:T(8,128)S(1)} %fusion.47, f32[1,8,32,4096]{3,1,2,0:T(8,128)S(1)} %copy_multiply_fusion, f32[1,8,32,4095]{3,1,2,0:T(8,128)} %get-tuple-element.43, f32[1,8,32,1]{3,1,2,0:T(8,128)} %get-tuple-element.45, f32[1,8,32,63]{3,1,2,0:T(8,128)S(1)} %get-tuple-element.39, ...), kind=kLoop, calls=%fused_computation.47 | loop fusion | flops 20971512 | bytes 25960480 | tf_op jit(solution)/shard_map/reduce_sum | solution.py:163
  153.6 5.3 %all_to_all.263 = f32[2,1,8]{2,1,0:T(1,128)S(1)} all-to-all(f32[2,1,8]{2,1,0:T(1,128)S(1)} %broadcast_in_dim.37), channel_id=1, replica_groups=mesh['dom'=8,'band'=8,'sub'=2] {'sub'}, dimensions={0} | all-to-all | bytes 128 | tf_op jit(solution)/shard_map/all_to_all | solution.py:54
  159.0 6.3 %fusion.26 = f32[1,32,4096]{2,0,1:T(1,128)S(1)} fusion(f32[1,8,32,4096]{3,1,2,0:T(8,128)} %get-tuple-element.15, f32[8]{0:T(128)S(1)} %add_sqrt_fusion.2, f32[1,8]{1,0:T(1,128)S(1)} %copy-done), kind=kOutput, calls=%fused_computation.38 | convolution fusion | flops 14680064 | bytes 4718656 | tf_op jit(solution)/shard_map/o,ozp->zp/dot_general | solution.py:111
  165.8 14.7 %all_to_all.264 = f32[8,4,4096]{2,1,0:T(4,128)S(1)} all-to-all(f32[8,4,4096]{2,1,0:T(4,128)S(1)} %reshape.548), channel_id=1, replica_groups=mesh['dom'=8,'band'=8,'sub'=2] {'band'}, dimensions={0} | all-to-all | bytes 1048576 | tf_op jit(solution)/shard_map/all_to_all | solution.py:26
  180.7 2.1 collective-permute-start.6
  182.8 3.4 collective-permute-start.7
  187.9 10.5 %all_to_all.265 = f32[16,1,768]{2,1,0:T(1,128)S(1)} all-to-all(f32[16,1,768]{2,1,0:T(1,128)S(1)} %reshape.571), channel_id=1, replica_groups=mesh['dom'=8,'band'=8,'sub'=2] {'band','sub'}, dimensions={0} | all-to-all | bytes 98304 | tf_op jit(solution)/shard_map/all_to_all | solution.py:133
  200.3 13.1 %all_to_all.266 = f32[8,1,1536]{2,1,0:T(1,128)S(1)} all-to-all(f32[8,1,1536]{2,1,0:T(1,128)S(1)} %reshape.573), channel_id=1, replica_groups=mesh['dom'=8,'band'=8,'sub'=2] {'dom'}, dimensions={0} | all-to-all | bytes 98304 | tf_op jit(solution)/shard_map/all_to_all | solution.py:137
  214.5 2.9 fusion.33
  217.4 2.9 convolution_bitcast_fusion.2
  221.4 9.0 %all_to_all.267 = f32[8,1,1536]{2,1,0:T(1,128)S(1)} all-to-all(f32[8,1,1536]{2,1,0:T(1,128)S(1)} %reshape.575), channel_id=1, replica_groups=mesh['dom'=8,'band'=8,'sub'=2] {'dom'}, dimensions={0} | all-to-all | bytes 98304 | tf_op jit(solution)/shard_map/all_to_all | solution.py:150
  233.3 11.3 %all_to_all.268 = f32[16,1,768]{2,1,0:T(1,128)S(1)} all-to-all(f32[16,1,768]{2,1,0:T(1,128)S(1)} %reshape.577), channel_id=1, replica_groups=mesh['dom'=8,'band'=8,'sub'=2] {'band','sub'}, dimensions={0} | all-to-all | bytes 98304 | tf_op jit(solution)/shard_map/all_to_all | solution.py:152
  246.6 4.7 %collective-permute-start.9 = (f32[4,8,64]{2,1,0:T(8,128)S(1)}, f32[4,8,64]{2,1,0:T(8,128)S(1)}, u32[]{:S(2)}, u32[]{:S(2)}) collective-permute-start(f32[4,8,64]{2,1,0:T(8,128)S(1)} %get-tuple-element.55), channel_id=1, source_target_pairs={{16,0},{32,16},{48,32},{64,48},{80,64},{96,80},{112,96},{0,112},{1... | collective-permute-start | bytes 24584 | tf_op jit(solution)/shard_map/ppermute | solution.py:39
  253.2 13.5 %all_to_all.269 = f32[8,1,16384]{2,1,0:T(1,128)S(1)} all-to-all(f32[8,1,16384]{2,1,0:T(1,128)S(1)} %reshape.579), channel_id=1, replica_groups=mesh['dom'=8,'band'=8,'sub'=2] {'band'}, dimensions={0} | all-to-all | bytes 1048576 | tf_op jit(solution)/shard_map/all_to_all | solution.py:54
  266.7 2.0 reduce.15
  269.5 2.8 broadcast_multiply_fusion.1
  272.5 3.7 fusion.191
  276.2 4.9 %fusion.190 = (f32[1,8,32,4033]{3,1,2,0:T(8,128)}, f32[1,8,32,4033]{3,1,2,0:T(8,128)}) fusion(f32[1,8,32,4096]{3,1,2,0:T(8,128)S(1)} %broadcast_multiply_fusion.1), kind=kLoop, calls=%fused_computation.262 | loop fusion | bytes 16519168 | tf_op jit(solution)/shard_map/jit(_roll_static)/slice | solution.py:82
  285.0 3.0 collective-permute-done.11
  288.0 10.3 %multiply_reduce_fusion.1 = (f32[8]{0:T(128)S(1)}, f32[1,8,32,4096]{3,1,2,0:T(8,128)}) fusion(f32[32,4096]{1,0:T(8,128)S(1)} %fusion.49, f32[1,8,32,4096]{3,1,2,0:T(8,128)S(1)} %broadcast_multiply_fusion.1, f32[1,8,32,4095]{3,1,2,0:T(8,128)} %get-tuple-element.33, f32[1,8,32,1]{3,1,2,0:T(8,128)} %get-tuple-element.35, ...), kind=kLoop, calls=%fused_computation.45 | loop fusion | flops 20971512 | bytes 25960480 | tf_op jit(solution)/shard_map/reduce_sum | solution.py:163
  298.3 5.3 %all_to_all.270 = f32[2,1,8]{2,1,0:T(1,128)S(1)} all-to-all(f32[2,1,8]{2,1,0:T(1,128)S(1)} %broadcast_in_dim.39), channel_id=1, replica_groups=mesh['dom'=8,'band'=8,'sub'=2] {'sub'}, dimensions={0} | all-to-all | bytes 128 | tf_op jit(solution)/shard_map/all_to_all | solution.py:54
  303.7 6.3 %fusion.24 = f32[1,32,4096]{2,0,1:T(1,128)S(1)} fusion(f32[1,8,32,4096]{3,1,2,0:T(8,128)} %get-tuple-element.13, f32[8]{0:T(128)S(1)} %add_sqrt_fusion.1, f32[1,8]{1,0:T(1,128)S(1)} %copy-done), kind=kOutput, calls=%fused_computation.36 | convolution fusion | flops 14680064 | bytes 4718656 | tf_op jit(solution)/shard_map/o,ozp->zp/dot_general | solution.py:111
  310.5 14.8 %all_to_all.271 = f32[8,4,4096]{2,1,0:T(4,128)S(1)} all-to-all(f32[8,4,4096]{2,1,0:T(4,128)S(1)} %reshape.550), channel_id=1, replica_groups=mesh['dom'=8,'band'=8,'sub'=2] {'band'}, dimensions={0} | all-to-all | bytes 1048576 | tf_op jit(solution)/shard_map/all_to_all | solution.py:26
  325.5 2.1 collective-permute-start.12
  327.6 3.4 collective-permute-start.13
  332.7 10.5 %all_to_all.272 = f32[16,1,768]{2,1,0:T(1,128)S(1)} all-to-all(f32[16,1,768]{2,1,0:T(1,128)S(1)} %reshape.581), channel_id=1, replica_groups=mesh['dom'=8,'band'=8,'sub'=2] {'band','sub'}, dimensions={0} | all-to-all | bytes 98304 | tf_op jit(solution)/shard_map/all_to_all | solution.py:133
  345.0 13.1 %all_to_all.273 = f32[8,1,1536]{2,1,0:T(1,128)S(1)} all-to-all(f32[8,1,1536]{2,1,0:T(1,128)S(1)} %reshape.583), channel_id=1, replica_groups=mesh['dom'=8,'band'=8,'sub'=2] {'dom'}, dimensions={0} | all-to-all | bytes 98304 | tf_op jit(solution)/shard_map/all_to_all | solution.py:137
  359.3 2.9 fusion.32
  362.2 2.9 convolution_bitcast_fusion
  366.2 9.0 %all_to_all.274 = f32[8,1,1536]{2,1,0:T(1,128)S(1)} all-to-all(f32[8,1,1536]{2,1,0:T(1,128)S(1)} %reshape.585), channel_id=1, replica_groups=mesh['dom'=8,'band'=8,'sub'=2] {'dom'}, dimensions={0} | all-to-all | bytes 98304 | tf_op jit(solution)/shard_map/all_to_all | solution.py:150
  378.0 11.3 %all_to_all.275 = f32[16,1,768]{2,1,0:T(1,128)S(1)} all-to-all(f32[16,1,768]{2,1,0:T(1,128)S(1)} %reshape.587), channel_id=1, replica_groups=mesh['dom'=8,'band'=8,'sub'=2] {'band','sub'}, dimensions={0} | all-to-all | bytes 98304 | tf_op jit(solution)/shard_map/all_to_all | solution.py:152
  391.4 4.7 %collective-permute-start.15 = (f32[4,8,64]{2,1,0:T(8,128)S(1)}, f32[4,8,64]{2,1,0:T(8,128)S(1)}, u32[]{:S(2)}, u32[]{:S(2)}) collective-permute-start(f32[4,8,64]{2,1,0:T(8,128)S(1)} %get-tuple-element.53), channel_id=1, source_target_pairs={{16,0},{32,16},{48,32},{64,48},{80,64},{96,80},{112,96},{0,112},{1... | collective-permute-start | bytes 24584 | tf_op jit(solution)/shard_map/ppermute | solution.py:39
  398.0 13.5 %all_to_all.276 = f32[8,1,16384]{2,1,0:T(1,128)S(1)} all-to-all(f32[8,1,16384]{2,1,0:T(1,128)S(1)} %reshape.589), channel_id=1, replica_groups=mesh['dom'=8,'band'=8,'sub'=2] {'band'}, dimensions={0} | all-to-all | bytes 1048576 | tf_op jit(solution)/shard_map/all_to_all | solution.py:54
  415.5 2.8 broadcast_multiply_fusion
  418.4 3.7 fusion.186
  422.1 4.8 %fusion.185 = (f32[1,8,32,4033]{3,1,2,0:T(8,128)}, f32[1,8,32,4033]{3,1,2,0:T(8,128)}) fusion(f32[1,8,32,4096]{3,1,2,0:T(8,128)S(1)} %broadcast_multiply_fusion), kind=kLoop, calls=%fused_computation.257 | loop fusion | bytes 16519168 | tf_op jit(solution)/shard_map/jit(_roll_static)/slice | solution.py:82
  428.5 2.3 collective-permute-done.16
  430.8 3.0 collective-permute-done.17
  433.8 10.3 %multiply_reduce_fusion = (f32[8]{0:T(128)S(1)}, f32[1,8,32,4096]{3,1,2,0:T(8,128)}) fusion(f32[32,4096]{1,0:T(8,128)S(1)} %fusion.51, f32[1,8,32,4096]{3,1,2,0:T(8,128)S(1)} %broadcast_multiply_fusion, f32[1,8,32,4095]{3,1,2,0:T(8,128)} %get-tuple-element.23, f32[1,8,32,1]{3,1,2,0:T(8,128)S(1)} %get-tuple-element.25, ...), kind=kLoop, calls=%fused_computation.43 | loop fusion | flops 20971512 | bytes 25960480 | tf_op jit(solution)/shard_map/reduce_sum | solution.py:163
  444.1 5.0 %all_to_all.277 = f32[2,1,8]{2,1,0:T(1,128)S(1)} all-to-all(f32[2,1,8]{2,1,0:T(1,128)S(1)} %broadcast_in_dim.41), channel_id=1, replica_groups=mesh['dom'=8,'band'=8,'sub'=2] {'sub'}, dimensions={0} | all-to-all | bytes 128 | tf_op jit(solution)/shard_map/all_to_all | solution.py:54
  449.0 2.7 broadcast_divide_fusion
  451.8 4.4 copy.229
  (178 shorter events, 60.5 us)
Async XLA Ops:
  0.6 5.3 %copy-start = (f32[1,8]{1,0:T(1,128)S(1)}, f32[1,8]{1,0:T(1,128)}, u32[]{:S(2)}) copy-start(f32[1,8]{1,0:T(1,128)} %param.5) | copy-start | bytes 100
  12.6 16.2 %all-to-all-start = ((f32[8,4,4096]{2,1,0:T(4,128)}), f32[8,4,4096]{2,1,0:T(4,128)S(1)}, u32[]{:S(2)}, u32[]{:S(2)}) async-start(f32[8,4,4096]{2,1,0:T(4,128)} %reshape.546), calls=%async_computation | async-start | bytes 1048576 | tf_op jit(solution)/shard_map/all_to_all | solution.py:26
  28.9 6.4 %collective-permute-start = (f32[4,8,64]{2,1,0:T(8,128)S(1)}, f32[4,8,64]{2,1,0:T(8,128)S(1)}, u32[]{:S(2)}, u32[]{:S(2)}) collective-permute-start(f32[4,8,64]{2,1,0:T(8,128)S(1)} %get-tuple-element.50), channel_id=1, source_target_pairs={{0,16},{16,32},{32,48},{48,64},{64,80},{80,96},{96,112},{112,0},{1... | collective-permute-start | bytes 24584 | tf_op jit(solution)/shard_map/ppermute | solution.py:37
  31.7 4.4 collective-permute-start.1
  37.4 11.4 %all-to-all-start.1 = ((f32[16,1,768]{2,1,0:T(1,128)}), f32[16,1,768]{2,1,0:T(1,128)S(1)}, u32[]{:S(2)}, u32[]{:S(2)}) async-start(f32[16,1,768]{2,1,0:T(1,128)} %reshape.561), calls=%async_computation.1 | async-start | bytes 98304 | tf_op jit(solution)/shard_map/all_to_all | solution.py:133
  51.8 13.2 %all-to-all-start.2 = ((f32[8,1,1536]{2,1,0:T(1,128)}), f32[8,1,1536]{2,1,0:T(1,128)S(1)}, u32[]{:S(2)}, u32[]{:S(2)}) async-start(f32[8,1,1536]{2,1,0:T(1,128)} %reshape.563), calls=%async_computation.2 | async-start | bytes 98304 | tf_op jit(solution)/shard_map/all_to_all | solution.py:137
  97.8 25.2 %copy-start.1 = (f32[1,32,4096]{2,1,0:T(8,128)S(1)}, f32[1,32,4096]{2,1,0:T(8,128)}, u32[]{:S(2)}) copy-start(f32[1,32,4096]{2,1,0:T(8,128)} %param.6) | copy-start | bytes 1572868
  97.8 6.3 %collective-permute-start.2 = (f32[4,8,64]{2,1,0:T(8,128)S(1)}, f32[4,8,64]{2,1,0:T(8,128)S(1)}, u32[]{:S(2)}, u32[]{:S(2)}) collective-permute-start(f32[4,8,64]{2,1,0:T(8,128)S(1)} %get-tuple-element.56), channel_id=1, source_target_pairs={{0,16},{16,32},{32,48},{48,64},{64,80},{80,96},{96,112},{112,0},{1... | collective-permute-start | bytes 24584 | tf_op jit(solution)/shard_map/ppermute | solution.py:37
  98.3 5.8 %collective-permute-start.3 = (f32[4,8,64]{2,1,0:T(8,128)S(1)}, f32[4,8,64]{2,1,0:T(8,128)S(1)}, u32[]{:S(2)}, u32[]{:S(2)}) collective-permute-start(f32[4,8,64]{2,1,0:T(8,128)S(1)} %get-tuple-element.57), channel_id=1, source_target_pairs={{16,0},{32,16},{48,32},{64,48},{80,64},{96,80},{112,96},{0,112},{1... | collective-permute-start | bytes 24584 | tf_op jit(solution)/shard_map/ppermute | solution.py:39
  105.6 14.5 %all-to-all-start.5 = ((f32[8,1,16384]{2,1,0:T(1,128)}), f32[8,1,16384]{2,1,0:T(1,128)S(1)}, u32[]{:S(2)}, u32[]{:S(2)}) async-start(f32[8,1,16384]{2,1,0:T(1,128)} %reshape.569), calls=%async_computation.5 | async-start | bytes 1048576 | tf_op jit(solution)/shard_map/all_to_all | solution.py:54
  136.3 3.9 collective-permute-start.4
  136.7 6.6 %collective-permute-start.5 = (f32[1,8,1,4096]{3,1,2,0:T(8,128)S(1)}, f32[1,8,1,4096]{3,1,2,0:T(8,128)}, u32[]{:S(2)}, u32[]{:S(2)}) collective-permute-start(f32[1,8,1,4096]{3,1,2,0:T(8,128)S(1)} %get-tuple-element.37), channel_id=1, source_target_pairs={{0,1},{1,0},{2,3},{3,2},{4,5},{5,4},{6,7},{7,6},{8,9},{9,8},{10,11... | collective-permute-start | bytes 393224 | tf_op jit(solution)/shard_map/ppermute | solution.py:37
  180.7 6.5 %collective-permute-start.6 = (f32[4,8,64]{2,1,0:T(8,128)S(1)}, f32[4,8,64]{2,1,0:T(8,128)S(1)}, u32[]{:S(2)}, u32[]{:S(2)}) collective-permute-start(f32[4,8,64]{2,1,0:T(8,128)S(1)} %get-tuple-element.48), channel_id=1, source_target_pairs={{0,16},{16,32},{32,48},{48,64},{64,80},{80,96},{96,112},{112,0},{1... | collective-permute-start | bytes 24584 | tf_op jit(solution)/shard_map/ppermute | solution.py:37
  182.8 4.4 collective-permute-start.7
  246.1 6.3 %collective-permute-start.8 = (f32[4,8,64]{2,1,0:T(8,128)S(1)}, f32[4,8,64]{2,1,0:T(8,128)S(1)}, u32[]{:S(2)}, u32[]{:S(2)}) collective-permute-start(f32[4,8,64]{2,1,0:T(8,128)S(1)} %get-tuple-element.54), channel_id=1, source_target_pairs={{0,16},{16,32},{32,48},{48,64},{64,80},{80,96},{96,112},{112,0},{1... | collective-permute-start | bytes 24584 | tf_op jit(solution)/shard_map/ppermute | solution.py:37
  246.6 5.8 %collective-permute-start.9 = (f32[4,8,64]{2,1,0:T(8,128)S(1)}, f32[4,8,64]{2,1,0:T(8,128)S(1)}, u32[]{:S(2)}, u32[]{:S(2)}) collective-permute-start(f32[4,8,64]{2,1,0:T(8,128)S(1)} %get-tuple-element.55), channel_id=1, source_target_pairs={{16,0},{32,16},{48,32},{64,48},{80,64},{96,80},{112,96},{0,112},{1... | collective-permute-start | bytes 24584 | tf_op jit(solution)/shard_map/ppermute | solution.py:39
  281.1 3.9 collective-permute-start.10
  281.5 6.5 %collective-permute-start.11 = (f32[1,8,1,4096]{3,1,2,0:T(8,128)S(1)}, f32[1,8,1,4096]{3,1,2,0:T(8,128)}, u32[]{:S(2)}, u32[]{:S(2)}) collective-permute-start(f32[1,8,1,4096]{3,1,2,0:T(8,128)S(1)} %get-tuple-element.27), channel_id=1, source_target_pairs={{0,1},{1,0},{2,3},{3,2},{4,5},{5,4},{6,7},{7,6},{8,9},{9,8},{10,11... | collective-permute-start | bytes 393224 | tf_op jit(solution)/shard_map/ppermute | solution.py:37
  325.5 6.5 %collective-permute-start.12 = (f32[4,8,64]{2,1,0:T(8,128)S(1)}, f32[4,8,64]{2,1,0:T(8,128)S(1)}, u32[]{:S(2)}, u32[]{:S(2)}) collective-permute-start(f32[4,8,64]{2,1,0:T(8,128)S(1)} %get-tuple-element.46), channel_id=1, source_target_pairs={{0,16},{16,32},{32,48},{48,64},{64,80},{80,96},{96,112},{112,0},{1... | collective-permute-start | bytes 24584 | tf_op jit(solution)/shard_map/ppermute | solution.py:37
  327.6 4.5 collective-permute-start.13
  390.9 6.3 %collective-permute-start.14 = (f32[4,8,64]{2,1,0:T(8,128)S(1)}, f32[4,8,64]{2,1,0:T(8,128)S(1)}, u32[]{:S(2)}, u32[]{:S(2)}) collective-permute-start(f32[4,8,64]{2,1,0:T(8,128)S(1)} %get-tuple-element.52), channel_id=1, source_target_pairs={{0,16},{16,32},{32,48},{48,64},{64,80},{80,96},{96,112},{112,0},{1... | collective-permute-start | bytes 24584 | tf_op jit(solution)/shard_map/ppermute | solution.py:37
  391.4 5.8 %collective-permute-start.15 = (f32[4,8,64]{2,1,0:T(8,128)S(1)}, f32[4,8,64]{2,1,0:T(8,128)S(1)}, u32[]{:S(2)}, u32[]{:S(2)}) collective-permute-start(f32[4,8,64]{2,1,0:T(8,128)S(1)} %get-tuple-element.53), channel_id=1, source_target_pairs={{16,0},{32,16},{48,32},{64,48},{80,64},{96,80},{112,96},{0,112},{1... | collective-permute-start | bytes 24584 | tf_op jit(solution)/shard_map/ppermute | solution.py:39
  427.0 3.8 collective-permute-start.16
  427.4 6.4 %collective-permute-start.17 = (f32[1,8,1,4096]{3,1,2,0:T(8,128)S(1)}, f32[1,8,1,4096]{3,1,2,0:T(8,128)S(1)}, u32[]{:S(2)}, u32[]{:S(2)}) collective-permute-start(f32[1,8,1,4096]{3,1,2,0:T(8,128)S(1)} %get-tuple-element.17), channel_id=1, source_target_pairs={{0,1},{1,0},{2,3},{3,2},{4,5},{5,4},{6,7},{7,6},{8,9},{9,8},{10,11... | collective-permute-start | bytes 393224 | tf_op jit(solution)/shard_map/ppermute | solution.py:37
where the time goes:
time: 465 us; the launch traced here: 456 us
  blocking collectives  180 us (39%)
  other arithmetic  63.7 us (14%)
  starting transfers between devices  60.1 us (13%)
  local copies, waits for them, and re-layouts  55.6 us (12%)
  waiting for transfers between devices  53.1 us (11%)
  matrix products  40.5 us (9%)
    all_to_all x5, blocking collectives, sent_to_all(): lax.all_to_all(jnp.broadcast_to(value[None], (length, *value.shape)), axi...  42.6 us
    all_to_all x3, blocking collectives, body(): lax.all_to_all(columns, ('band', 'sub'), split_axis=0, concat_axis=2, til...  34 us
    reduce_sum x3, other arithmetic, body(): squares = taken_together(jnp.sum(stepped * stepped, axis=(2, 3)), 'sub')  30.8 us
    all_to_all x2, blocking collectives, summed_on_arrival(): lax.all_to_all(blocks, axis, split_axis=0, concat_axis=0, tiled=True)  29.5 us
    all_to_all x3, blocking collectives, body(): lax.all_to_all(lengthwise, 'dom', split_axis=1, concat_axis=0, tiled=True)  27.1 us
    all_to_all x2, blocking collectives, body(): lax.all_to_all(columns, 'dom', split_axis=0, concat_axis=1, tiled=True)  26.2 us
    ppermute x9, starting transfers between devices, with_halo(): lax.ppermute(head, axis, [((i + 1) % count, i) for i in range(count)])  24.4 us
    all_to_all x2, blocking collectives, body(): lax.all_to_all(spectrum_y, ('band', 'sub'), split_axis=2, concat_axis=0,...  20.9 us
  transfers between devices with their start and end apart: 22, of which 17 were waited for; matrix products, arithmetic and copies ran while one was open for 0% of the time, Pallas kernels for 0%

commit v1 on v0

v1 whole, which is shorter than its diff:
```python
import functools

import jax
import jax.numpy as jnp
import numpy as np
from jax import lax
from jax.experimental import pallas as pl
from jax.experimental.pallas import tpu as pltpu
from jax.sharding import PartitionSpec as P

EDGE = 64
MARGIN = 8
BLOCK = 4
STEPS = 3
CORE = 48
GX = 384
N_DOM = 8
N_BAND = 8
TIME = 0.2
SCREEN = 0.02
EPS = 1e-06
CELLS = float(EDGE**3)
F32 = jnp.float32
HIGH = lax.Precision.HIGH
MESH = pl.DeviceIdType.MESH


def cas(rows, cols, n):
    angle = 2.0 * np.pi / n * ((rows[:, None] * cols[None, :]) % n)
    return np.cos(angle) + np.sin(angle)


def tables():
    ids = np.arange(EDGE)
    full = cas(ids, ids, EDGE)
    w_y = np.kron(np.eye(2), full)
    w_h = np.concatenate([np.concatenate([full, full], 1), np.zeros((64, 128))], 0)
    w_z = np.kron(np.eye(4), np.concatenate([full[:32], full[:32]], 1))
    both = np.concatenate([full, full], 0)
    halo0 = np.tile(both[:, [63, 32]], (1, 16))
    halo1 = np.tile(both[:, [31, 0]], (1, 16))
    w_i = np.concatenate(
        [np.kron(np.eye(4), b) for b in (both[:, :32], both[:, 32:], halo0, halo1)], 1
    )
    lam = 2.0 - 2.0 * np.cos(2.0 * np.pi / EDGE * ids)
    a = lam[:, None] + lam[None, :] + SCREEN
    r = 1.0 / (1.0 + a / 2 + np.sqrt(a + a * a / 4))
    scale = 1.0 / (1.0 / r - r) / (EDGE * EDGE)
    sign = np.where(ids % 2 == 1, -1.0, 1.0)[None, :]
    rows = [r, scale, scale * sign]
    for k in range(2, 10):
        rows.append(r ** (CORE * k - 63) / (1.0 - r**GX))
    modes = np.stack(rows)
    modes = np.concatenate([modes, modes], 2).reshape(11, N_BAND, 8, 128).transpose(1, 0, 2, 3)
    return [np.asarray(v, np.float32) for v in (w_y, w_h, w_z, w_i, modes)]


def dot(a, b, dims=((1,), (0,))):
    return lax.dot_general(a, b, (dims, ((), ())), precision=HIGH, preferred_element_type=F32)


def kernel(
    orb_hbm, occ, ext_hbm, core, wy_hbm, wh_hbm, wz_hbm, wi_hbm, modes_hbm,
    out_hbm, pot_hbm, inv_out,
    U, HALF, EXT, VB, WY, WH, WZ, WI, MODES, OCC8, W8, INV,
    SB, RA, S1, RB, S2, PP, PW, FS, FR, MV, QB, OB, R4, AG, EDGES, ER, EXTE, EXTR, HH, SH, NBO, NB, NR,
    l_u, l_c, ssA, rsA, ssB, rsB, ssF, rsF, ssM, rsM, ss4, rs4, ssG, rsG, ssH, rsH, ssE, rsE,
    ssX, rsX, ssN, rsN, l_o,
):
    d = lax.axis_index("dom")
    b = lax.axis_index("band")
    h = lax.axis_index("sub")
    zi = b // 2
    co = b % 2
    mate = zi * 2 + (1 - co)
    other = 1 - h

    def zpeer(k):
        return ((zi + k) % 4) * 2 + co

    loads = [pltpu.make_async_copy(orb_hbm.at[0, o], U.at[o], l_u.at[o]) for o in range(8)]
    loads += [
        pltpu.make_async_copy(src, dst, l_c.at[i])
        for i, (src, dst) in enumerate(
            (
                (ext_hbm.at[0], EXT),
                (wy_hbm, WY),
                (wh_hbm, WH),
                (wz_hbm, WZ),
                (wi_hbm, WI),
                (modes_hbm.at[b], MODES),
            )
        )
    ]
    for c in loads:
        c.start()

    barrier = pltpu.get_barrier_semaphore()

    def greet(dev):
        pl.semaphore_signal(barrier, inc=1, device_id=dev, device_id_type=MESH)

    greet({"band": mate})
    for k in range(1, 4):
        greet({"band": zpeer(k)})
    greet({"sub": other})
    for k in range(1, 8):
        greet({"dom": (d + k) % 8})

    def send(src, dst, ss, rs, dev):
        return pltpu.make_async_remote_copy(
            src_ref=src, dst_ref=dst, send_sem=ss, recv_sem=rs, device_id=dev, device_id_type=MESH
        )

    lane = lax.broadcasted_iota(jnp.int32, (8, 128), 1)
    low = lane < 64
    lane16 = lax.broadcasted_iota(jnp.int32, (16, 128), 1)
    lane32 = lax.broadcasted_iota(jnp.int32, (32, 128), 1)
    row32 = lax.broadcasted_iota(jnp.int32, (32, 128), 0)
    low32 = lane32 < 64
    first_y = (lane32 == 0) | (lane32 == 64)
    last_y = (lane32 == 63) | (lane32 == 127)
    slot = (lane % 32) // 2
    zero8 = jnp.zeros((8, 128), F32)

    for o in range(8):
        OCC8[o : o + 1, :] = jnp.full((1, 128), occ[0, o], F32)
    W8[...] = OCC8[...]
    INV[...] = jnp.ones((8, 8, 128), F32)

    for c in loads:
        c.wait()

    r = MODES[0]
    power = jnp.ones((8, 128), F32)
    for i in range(64):
        PW[i] = power
        power = power * r

    def lanes(tile):
        return pl.ds(tile * 128, 128)

    for tile in range(32):
        EXTE[0, tile : tile + 1, :] = EXT[31:32, lanes(tile)]
        EXTE[1, tile : tile + 1, :] = EXT[0:1, lanes(tile)]

    def first_edges(o, carry):
        for tile in range(32):
            EDGES[0, 0, o, tile : tile + 1, :] = U[o, 31:32, lanes(tile)]
            EDGES[0, 1, o, tile : tile + 1, :] = U[o, 0:1, lanes(tile)]
        return carry

    lax.fori_loop(0, 8, first_edges, 0)

    pl.semaphore_wait(barrier, 12)

    ext_copy = send(EXTE, EXTR, ssX.at[0], rsX.at[0], {"sub": other})
    ext_copy.start()

    low_x = core[0, 0] * BLOCK
    high_x = core[0, 1] * BLOCK

    def step(st, carry):
        edge_copy = send(EDGES.at[st], ER.at[st], ssE.at[st], rsE.at[st], {"sub": other})
        edge_copy.start()

        for g in range(8):
            tiles = []
            for t in range(4):
                tile = 4 * g + t
                acc = jnp.zeros((32, 128), F32)
                for o in range(8):
                    value = U[o, :, lanes(tile)]
                    acc = acc + value * value * W8[o : o + 1, :]
                x = 2 * tile + lane32 // 64
                tiles.append(jnp.where((x >= low_x) & (x < high_x), acc, 0.0))
            rho = jnp.concatenate(tiles, 0)
            out = dot(WY[...], rho, ((1,), (1,)))
            for x2 in range(2):
                for c in range(2):
                    for z in range(4):
                        row = x2 * 64 + (2 * z + c) * 8
                        SB[c, z, 2 * g + x2] = out[row : row + 8]

        copy_a = send(SB.at[1 - co], RA.at[st], ssA.at[st], rsA.at[st], {"band": mate})
        copy_a.start()
        copy_a.wait_recv()
        copies_b = []
        for k in range(1, 4):
            z = (zi + k) % 4
            S1[k] = SB[co, z] + RA[st, z]
            copy = send(
                S1.at[k], RB.at[st, k - 1], ssB.at[st, k - 1], rsB.at[st, k - 1], {"band": zpeer(k)}
            )
            copy.start()
            copies_b.append(copy)
        S1[0] = SB[co, zi] + RA[st, zi]
        for copy in copies_b:
            copy.wait_recv()
        total = S1[0] + RB[st, 0] + RB[st, 1] + RB[st, 2]

        out = dot(total.reshape(128, 128), WZ[...])
        scale = MODES[1 + h]
        r = MODES[0]
        for g in range(8):
            for t in range(4):
                for x2 in range(2):
                    row = (2 * g + x2) * 8
                    S2[8 * g + 2 * t + x2] = out[row : row + 8, t * 128 : t * 128 + 128] * scale

        p = zero8
        for i in range(64):
            p = p * r + jnp.where(low, S2[i], S2[63 - i])
            PP[i] = p
        MV[st, d] = p
        moment_copies = []
        for k in range(1, 8):
            copy = send(
                MV.at[st, d], MV.at[st, d], ssM.at[st, k - 1], rsM.at[st, k - 1], {"dom": (d + k) % 8}
            )
            copy.start()
            moment_copies.append(copy)

        def response(x):
            return jnp.where(low, PP[x] - S2[x], PP[63 - x])

        side_copies = []
        for side, base, peer in ((0, 48, (d + 1) % 8), (1, 0, (d + 7) % 8)):
            for m in range(8):
                even = response(base + 2 * m)
                odd = response(base + 2 * m + 1)
                even = even + pltpu.roll(even, 64, 1)
                odd = odd + pltpu.roll(odd, 64, 1)
                FS[side, m] = jnp.where(low, even, odd)
            copy = send(
                FS.at[side], FR.at[st, side], ssF.at[st, side], rsF.at[st, side], {"dom": peer}
            )
            copy.start()
            side_copies.append(copy)

        for copy in moment_copies:
            copy.wait_recv()
        for copy in side_copies:
            copy.wait_recv()

        incoming = zero8
        for k in range(2, 10):
            moved = jnp.where(low, MV[st, (d + 16 - k) % 8], MV[st, (d + k) % 8])
            incoming = incoming + MODES[1 + k] * moved
        near = jnp.where(low, MV[st, (d + 7) % 8], MV[st, (d + 1) % 8])
        for i in range(64):
            value = PP[i] + PW[i] * incoming
            if i >= 16:
                value = value + PW[i - 15] * near
            PP[i] = value
        for x in range(64):
            value = response(x)
            if x < 16:
                part = FR[st, 0, x // 2]
                value = value + jnp.where(low if x % 2 == 0 else ~low, part, 0.0)
            if x >= 48:
                part = FR[st, 1, (x - 48) // 2]
                value = value + jnp.where(low if x % 2 == 0 else ~low, part, 0.0)
            g, t, x2 = x // 8, (x % 8) // 2, x % 2
            row = (2 * g + x2) * 8
            QB[row : row + 8, t * 128 : t * 128 + 128] = value

        out = dot(QB[...], WI[...])
        for q in range(2):
            halo = zero8
            for g in range(8):
                for x2 in range(2):
                    j = 2 * g + x2
                    OB[q, j] = out[j * 8 : j * 8 + 8, q * 128 : q * 128 + 128]
                    part = out[j * 8 : j * 8 + 8, (2 + q) * 128 : (2 + q) * 128 + 128]
                    halo = jnp.where(slot == x2 * 8 + g, part, halo)
            OB[q, 16] = halo
        copy_4 = send(OB.at[other], R4.at[st], ss4.at[st], rs4.at[st], {"sub": other})
        copy_4.start()
        copy_4.wait_recv()
        AG[st, b] = OB[h] + R4[st]

        gather = []
        for k in range(1, 4):
            copy = send(
                AG.at[st, b], AG.at[st, b], ssG.at[st, k - 1], rsG.at[st, k - 1], {"band": zpeer(k)}
            )
            copy.start()
            gather.append(copy)
        forward = [send(AG.at[st, b], AG.at[st, b], ssH.at[st, 0], rsH.at[st, 0], {"band": mate})]
        forward[0].start()
        for k in range(1, 4):
            gather[k - 1].wait_recv()
            came = zpeer(4 - k)
            copy = send(
                AG.at[st, came], AG.at[st, came], ssH.at[st, k], rsH.at[st, k], {"band": mate}
            )
            copy.start()
            forward.append(copy)
        for copy in forward:
            copy.wait_recv()

        for g in range(8):
            parts = [AG[st, :, 2 * g + x2].reshape(64, 128) for x2 in range(2)]
            cols = jnp.concatenate(parts, 0).T
            out = dot(cols, WY[...])
            for t in range(4):
                tile = 4 * g + t
                value = out[t * 32 : t * 32 + 32]
                VB[:, lanes(tile)] = value
                HALF[:, lanes(tile)] = jnp.exp(-0.5 * TIME * (value + EXT[:, lanes(tile)]))

        @pl.when(st == 0)
        def _():
            ext_copy.wait()

        edge_copy.wait_recv()
        rims = AG[st, :, 16].reshape(64, 128)
        out = dot(jnp.concatenate([rims, rims], 0).T, WH[...])
        low16 = lane16 < 64
        for t in range(4):
            value = jnp.where(low16, out[t * 32 : t * 32 + 16], out[t * 32 + 16 : t * 32 + 32])
            for g in range(8):
                tile = 4 * g + t
                for q in range(2):
                    HH[q, tile : tile + 1, :] = value[2 * g + q : 2 * g + q + 1]
        for q in range(2):
            half = jnp.exp(-0.5 * TIME * (HH[q] + EXTR[q]))
            for o in range(8):
                SH[q, o] = ER[st, q, o] * half * INV[o, 0:1, :]

        def advance(o, carry):
            inv = INV[o, 0:1, :]

            def scaled(tile):
                return U[o, :, lanes(tile)] * HALF[:, lanes(tile)] * inv

            squares = jnp.zeros((32, 128), F32)
            before = jnp.zeros((32, 128), F32)
            here = scaled(0)
            turned = pltpu.roll(here, 64, 1)
            for tile in range(32):
                if tile < 31:
                    later = scaled(tile + 1)
                    after = pltpu.roll(later, 64, 1)
                else:
                    later = here
                    after = jnp.zeros((32, 128), F32)
                next_y = pltpu.roll(jnp.where(first_y, turned, here), 127, 1)
                prior_y = pltpu.roll(jnp.where(last_y, turned, here), 1, 1)
                prior_z = jnp.where(
                    row32 == 0, SH[0, o, tile : tile + 1, :], pltpu.roll(here, 1, 0)
                )
                next_z = jnp.where(
                    row32 == 31, SH[1, o, tile : tile + 1, :], pltpu.roll(here, 31, 0)
                )
                around = turned + jnp.where(low32, before, after) + next_y + prior_y
                around = around + prior_z + next_z
                kept = 1.0 - 3.0 * TIME
                value = (kept * here + 0.5 * TIME * around) * HALF[:, lanes(tile)]
                U[o, :, lanes(tile)] = value
                EDGES[st + 1, 0, o, tile : tile + 1, :] = value[31:32]
                EDGES[st + 1, 1, o, tile : tile + 1, :] = value[0:1]
                squares = squares + value * value
                before, here, turned = turned, later, after
            NBO[o] = squares[0:8] + squares[8:16] + squares[16:24] + squares[24:32]

            @pl.when(st == STEPS - 1)
            def _():
                pltpu.make_async_copy(U.at[o], out_hbm.at[0, o], l_o.at[o]).start()

            return carry

        lax.fori_loop(0, 8, advance, 0)

        for o in range(8):
            NB[st, o : o + 1, :] = jnp.sum(NBO[o], axis=0, keepdims=True)
        norm_copy = send(NB.at[st], NR.at[st], ssN.at[st], rsN.at[st], {"sub": other})
        norm_copy.start()
        copy_a.wait_send()
        for copy in copies_b + moment_copies + side_copies + gather + forward + [copy_4, edge_copy]:
            copy.wait_send()
        norm_copy.wait()
        norms = jnp.sum(NB[st] + NR[st], axis=1, keepdims=True)
        inv = jnp.broadcast_to(1.0 / jnp.sqrt(norms / CELLS + EPS), (8, 128))
        for o in range(8):
            INV[o] = jnp.broadcast_to(inv[o : o + 1], (8, 128))
        W8[...] = OCC8[...] * inv * inv
        return carry

    lax.fori_loop(0, STEPS, step, 0)
    for o in range(8):
        inv_out[o : o + 1, :] = INV[o, 0:1, :]
    last = pltpu.make_async_copy(VB, pot_hbm.at[0], l_o.at[8])
    last.start()
    for o in range(8):
        pltpu.make_async_copy(U.at[o], out_hbm.at[0, o], l_o.at[o]).wait()
    last.wait()


def body(orbitals, occupations, ext_potential, core_range):
    consts = tables()
    hbm = pl.BlockSpec(memory_space=pl.ANY)
    smem = pl.BlockSpec(memory_space=pltpu.SMEM)
    vmem = pl.BlockSpec(memory_space=pltpu.VMEM)
    V = lambda *s: pltpu.VMEM(s, F32)
    D = lambda *s: pltpu.SemaphoreType.DMA(s)
    out, pot, inv = pl.pallas_call(
        kernel,
        out_shape=(
            jax.ShapeDtypeStruct(orbitals.shape, F32),
            jax.ShapeDtypeStruct(ext_potential.shape, F32),
            jax.ShapeDtypeStruct((8, 128), F32),
        ),
        in_specs=[hbm, smem, hbm, smem] + [hbm] * 5,
        out_specs=(hbm, hbm, vmem),
        scratch_shapes=[
            V(8, 32, 4096), V(32, 4096), V(32, 4096), V(32, 4096),
            V(128, 128), V(128, 128), V(128, 512), V(512, 512), V(11, 8, 128),
            V(8, 128), V(8, 128), V(8, 8, 128),
            V(2, 4, 16, 8, 128), V(3, 4, 16, 8, 128), V(4, 16, 8, 128), V(3, 3, 16, 8, 128),
            V(64, 8, 128), V(64, 8, 128), V(64, 8, 128),
            V(2, 8, 8, 128), V(3, 2, 8, 8, 128), V(3, 8, 8, 128), V(128, 512),
            V(2, 17, 8, 128), V(3, 17, 8, 128), V(3, 8, 17, 8, 128),
            V(4, 2, 8, 32, 128), V(3, 2, 8, 32, 128), V(2, 32, 128), V(2, 32, 128), V(2, 32, 128),
            V(2, 8, 32, 128), V(8, 8, 128), V(3, 8, 128), V(3, 8, 128),
            D(8), D(6), D(3), D(3), D(3, 3), D(3, 3), D(3, 2), D(3, 2), D(3, 7), D(3, 7),
            D(3), D(3), D(3, 3), D(3, 3), D(3, 4), D(3, 4), D(3), D(3), D(1), D(1), D(3), D(3), D(9),
        ],
        compiler_params=pltpu.CompilerParams(
            collective_id=0, has_side_effects=True, vmem_limit_bytes=60 * 1024 * 1024
        ),
        name="steps",
    )(orbitals, occupations, ext_potential, core_range, *[jnp.asarray(c) for c in consts])
    return out * inv[:, 0][None, :, None, None], pot


def solution(mesh):
    return jax.shard_map(
        body,
        mesh=mesh,
        in_specs=(
            P("dom", "band", "sub", None),
            P("dom", "band"),
            P("dom", "sub", None),
            P("dom", None),
        ),
        out_specs=(P("dom", "band", "sub", None), P("dom", "sub", None)),
        check_vma=False,
    )
```

time: 465 us -> 120 us (0.26); the launches traced: 456 us -> 120 us
  blocking collectives: 180 us -> 0 us
  Pallas kernels: 0 us -> 113 us
  starting transfers between devices: 60.1 us -> 0 us
  other arithmetic: 63.7 us -> 4.82 us
  local copies, waits for them, and re-layouts: 55.6 us -> 1.58 us
  waiting for transfers between devices: 53.1 us -> 0 us
  matrix products: 40.5 us -> 0 us
    all_to_all x17 -> x0, blocking collectives: 180 us -> none  [the longest x5 42.6 us: sent_to_all(): lax.all_to_all(jnp.broadcast_to(value[None], (length, *value.shape)), axi...]
    pallas_call x0 -> x1, Pallas kernels: none -> 113 us  [body(): pl.pallas_call(kernel, out_shape=(jax.ShapeDtypeStruct(orbitals.shape, F3...]
    dot_general x21 -> x0, matrix products: 40.5 us -> none  [the longest x3 18.1 us: body(): jnp.einsum('o,ozp->zp', occupations[0], orbitals[0] * orbitals[0], precis...]
    ppermute x18 -> x0, starting transfers between devices: 36.2 us -> none  [the longest x9 24.4 us: with_halo(): lax.ppermute(head, axis, [((i + 1) % count, i) for i in range(count)])]
    reduce_sum x9 -> x0, other arithmetic: 31.1 us -> none  [the longest x3 30.8 us: body(): squares = taken_together(jnp.sum(stepped * stepped, axis=(2, 3)), 'sub')]
    all_to_all x4 -> x0, waiting for transfers between devices: 31.1 us -> none  [the longest x1 9.32 us: sent_to_all(): lax.all_to_all(jnp.broadcast_to(value[None], (length, *value.shape)), axi...]
    slice x22 -> x1, local copies, waits for them, and re-layouts: 29.1 us -> 0.79 us  [body(): return (out * inv[:, 0][None, :, None, None], pot)]
    all_to_all x4 -> x0, starting transfers between devices: 24 us -> none  [the longest x1 6.8 us: summed_on_arrival(): lax.all_to_all(blocks, axis, split_axis=0, concat_axis=0, tiled=True)]
  transfers between devices with their start and end apart: 22 -> 0, of which waited for: 17 -> 0; matrix products, arithmetic and copies ran while one was open for 0% -> 0% of each run, Pallas kernels for 0% -> 0%
where the time goes in v1:
time: 120 us
  Pallas kernels  113 us (94%)
  other arithmetic  4.82 us (4%)
  local copies, waits for them, and re-layouts  1.58 us (1%)
    pallas_call x1, Pallas kernels, body(): pl.pallas_call(kernel, out_shape=(jax.ShapeDtypeStruct(orbitals.shape, F3...  113 us
    mul x1, other arithmetic, body(): return (out * inv[:, 0][None, :, None, None], pot)  4.82 us

profile of v1, /device:TPU:1, one launch (start us, length us, event | category | flops | bytes accessed | tf_op | source)
XLA Modules:
  0.0 120.2 jit_solution(3157806106053163010)
XLA Ops:
  0.6 113.2 %steps.1 = (f32[1,8,32,4096]{3,2,1,0:T(8,128)}, f32[1,32,4096]{2,1,0:T(8,128)}, f32[8,128]{1,0:T(8,128)}) custom-call(f32[1,8,32,4096]{3,2,1,0:T(8,128)} %orb_hbm.1, f32[1,8]{1,0:T(1,128)} %occ.1, f32[1,32,4096]{2,1,0:T(8,128)} %ext_hbm.1, s32[1,2]{1,0:T(1,128)} %core.1, f32[128,128]{1,0:T(8,128)} %constant.10.clone.wy_hbm, ...), custom_call_target="tpu_custom_call" | custom-call | tf_op jit(solution)/shard_map/steps/pallas_call | solution.py:408
  113.8 0.8 slice_reduce_fusion
  114.6 0.0 copy-start
  114.6 4.8 %broadcast_multiply_fusion = f32[1,8,32,4096]{3,2,1,0:T(8,128)} fusion(f32[1,8,32,4096]{3,2,1,0:T(8,128)} %get-tuple-element.5, f32[8]{0:T(128)S(1)} %slice_reduce_fusion), kind=kLoop, calls=%fused_computation | loop fusion | flops 1048576 | bytes 8388640 | tf_op jit(solution)/shard_map/mul | solution.py:435
  119.4 0.0 copy-done
  119.4 0.8 copy.12
Async XLA Ops:
  114.6 4.8 %copy-start = (f32[1,32,4096]{2,1,0:T(8,128)S(1)}, f32[1,32,4096]{2,1,0:T(8,128)}, u32[]{:S(2)}) copy-start(f32[1,32,4096]{2,1,0:T(8,128)} %get-tuple-element.11) | copy-start | bytes 1572868

commit v2 on v1

--- a/solution.py
+++ b/solution.py
@@ -52,7 +52,12 @@
         rows.append(r ** (CORE * k - 63) / (1.0 - r**GX))
     modes = np.stack(rows)
     modes = np.concatenate([modes, modes], 2).reshape(11, N_BAND, 8, 128).transpose(1, 0, 2, 3)
-    return [np.asarray(v, np.float32) for v in (w_y, w_h, w_z, w_i, modes)]
+    swap = np.kron(1.0 - np.eye(2), np.eye(64))
+    ring = np.roll(np.eye(64), 1, 0) + np.roll(np.eye(64), -1, 0)
+    stencil = np.concatenate([np.kron(np.eye(2), ring) + swap, swap], 1)
+    stencil = np.concatenate([stencil, stencil], 0)
+    out = [np.asarray(v, np.float32) for v in (w_y, w_h, w_z, w_i, modes)]
+    return out + [np.asarray(stencil, jnp.bfloat16)]
 
 
 def dot(a, b, dims=((1,), (0,))):
@@ -60,12 +65,12 @@
 
 
 def kernel(
-    orb_hbm, occ, ext_hbm, core, wy_hbm, wh_hbm, wz_hbm, wi_hbm, modes_hbm,
-    out_hbm, pot_hbm, inv_out,
-    U, HALF, EXT, VB, WY, WH, WZ, WI, MODES, OCC8, W8, INV,
+    orb_hbm, occ, ext_hbm, core, wy_hbm, wh_hbm, wz_hbm, wi_hbm, modes_hbm, st_hbm,
+    U, VB, INV,
+    HALF, EXT, WY, WH, WZ, WI, MODES, WS, OCC8, W8, SC, MX,
     SB, RA, S1, RB, S2, PP, PW, FS, FR, MV, QB, OB, R4, AG, EDGES, ER, EXTE, EXTR, HH, SH, NBO, NB, NR,
     l_u, l_c, ssA, rsA, ssB, rsB, ssF, rsF, ssM, rsM, ss4, rs4, ssG, rsG, ssH, rsH, ssE, rsE,
-    ssX, rsX, ssN, rsN, l_o,
+    ssX, rsX, ssN, rsN,
 ):
     d = lax.axis_index("dom")
     b = lax.axis_index("band")
@@ -78,17 +83,18 @@
     def zpeer(k):
         return ((zi + k) % 4) * 2 + co
 
-    loads = [pltpu.make_async_copy(orb_hbm.at[0, o], U.at[o], l_u.at[o]) for o in range(8)]
+    loads = [pltpu.make_async_copy(orb_hbm.at[0, o], U.at[0, o], l_u.at[o]) for o in range(8)]
     loads += [
         pltpu.make_async_copy(src, dst, l_c.at[i])
         for i, (src, dst) in enumerate(
             (
+                (wy_hbm, WY),
                 (ext_hbm.at[0], EXT),
-                (wy_hbm, WY),
                 (wh_hbm, WH),
                 (wz_hbm, WZ),
                 (wi_hbm, WI),
                 (modes_hbm.at[b], MODES),
+                (st_hbm, WS),
             )
         )
     ]
@@ -116,10 +122,9 @@
     low = lane < 64
     lane16 = lax.broadcasted_iota(jnp.int32, (16, 128), 1)
     lane32 = lax.broadcasted_iota(jnp.int32, (32, 128), 1)
-    row32 = lax.broadcasted_iota(jnp.int32, (32, 128), 0)
-    low32 = lane32 < 64
-    first_y = (lane32 == 0) | (lane32 == 64)
-    last_y = (lane32 == 63) | (lane32 == 127)
+    row8 = lax.broadcasted_iota(jnp.int32, (8, 128), 0)
+    top = row8 == 0
+    bottom = row8 == 7
     slot = (lane % 32) // 2
     zero8 = jnp.zeros((8, 128), F32)
 
@@ -128,49 +133,30 @@
     W8[...] = OCC8[...]
     INV[...] = jnp.ones((8, 8, 128), F32)
 
-    for c in loads:
-        c.wait()
-
-    r = MODES[0]
-    power = jnp.ones((8, 128), F32)
-    for i in range(64):
-        PW[i] = power
-        power = power * r
-
     def lanes(tile):
         return pl.ds(tile * 128, 128)
 
-    for tile in range(32):
-        EXTE[0, tile : tile + 1, :] = EXT[31:32, lanes(tile)]
-        EXTE[1, tile : tile + 1, :] = EXT[0:1, lanes(tile)]
-
-    def first_edges(o, carry):
-        for tile in range(32):
-            EDGES[0, 0, o, tile : tile + 1, :] = U[o, 31:32, lanes(tile)]
-            EDGES[0, 1, o, tile : tile + 1, :] = U[o, 0:1, lanes(tile)]
-        return carry
-
-    lax.fori_loop(0, 8, first_edges, 0)
-
-    pl.semaphore_wait(barrier, 12)
-
-    ext_copy = send(EXTE, EXTR, ssX.at[0], rsX.at[0], {"sub": other})
-    ext_copy.start()
-
     low_x = core[0, 0] * BLOCK
     high_x = core[0, 1] * BLOCK
 
-    def step(st, carry):
-        edge_copy = send(EDGES.at[st], ER.at[st], ssE.at[st], rsE.at[st], {"sub": other})
-        edge_copy.start()
-
+    def to_mate(st, half):
+        part = pl.ds(8 * half, 8)
+        return send(
+            SB.at[1 - co, :, part], RA.at[st, :, part], ssA.at[st, half], rsA.at[st, half],
+            {"band": mate},
+        )
+
+    def edges_of(st):
+        return send(EDGES.at[st], ER.at[st], ssE.at[st], rsE.at[st], {"sub": other})
+
+    def density(st, first):
         for g in range(8):
             tiles = []
             for t in range(4):
                 tile = 4 * g + t
                 acc = jnp.zeros((32, 128), F32)
                 for o in range(8):
-                    value = U[o, :, lanes(tile)]
+                    value = U[0, o, :, lanes(tile)]
                     acc = acc + value * value * W8[o : o + 1, :]
                 x = 2 * tile + lane32 // 64
                 tiles.append(jnp.where((x >= low_x) & (x < high_x), acc, 0.0))
@@ -181,20 +167,56 @@
                     for z in range(4):
                         row = x2 * 64 + (2 * z + c) * 8
                         SB[c, z, 2 * g + x2] = out[row : row + 8]
-
-        copy_a = send(SB.at[1 - co], RA.at[st], ssA.at[st], rsA.at[st], {"band": mate})
-        copy_a.start()
-        copy_a.wait_recv()
+            if g == 3 and first:
+                pl.semaphore_wait(barrier, 12)
+            if g % 4 == 3:
+                to_mate(st, g // 4).start()
+
+    for c in loads[:9]:
+        c.wait()
+    density(0, True)
+    for c in loads[9:]:
+        c.wait()
+
+    for tile in range(32):
+        EXTE[0, tile : tile + 1, :] = EXT[31:32, lanes(tile)]
+        EXTE[1, tile : tile + 1, :] = EXT[0:1, lanes(tile)]
+
+    def first_edges(o, carry):
+        for tile in range(32):
+            EDGES[0, 0, o, tile : tile + 1, :] = U[0, o, 31:32, lanes(tile)]
+            EDGES[0, 1, o, tile : tile + 1, :] = U[0, o, 0:1, lanes(tile)]
+        return carry
+
+    lax.fori_loop(0, 8, first_edges, 0)
+    ext_copy = send(EXTE, EXTR, ssX.at[0], rsX.at[0], {"sub": other})
+    ext_copy.start()
+    edges_of(0).start()
+
+    r = MODES[0]
+    power = jnp.ones((8, 128), F32)
+    for i in range(64):
+        PW[i] = power
+        power = power * r
+
+    def step(st, carry):
+        edge_copy = edges_of(st)
+
+        copies_a = [to_mate(st, half) for half in range(2)]
         copies_b = []
-        for k in range(1, 4):
-            z = (zi + k) % 4
-            S1[k] = SB[co, z] + RA[st, z]
-            copy = send(
-                S1.at[k], RB.at[st, k - 1], ssB.at[st, k - 1], rsB.at[st, k - 1], {"band": zpeer(k)}
-            )
-            copy.start()
-            copies_b.append(copy)
-        S1[0] = SB[co, zi] + RA[st, zi]
+        for half in range(2):
+            part = pl.ds(8 * half, 8)
+            copies_a[half].wait_recv()
+            for k in (2, 1, 3):
+                z = (zi + k) % 4
+                S1[k, part] = SB[co, z, part] + RA[st, z, part]
+                copy = send(
+                    S1.at[k, part], RB.at[st, k - 1, part], ssB.at[st, k - 1, half],
+                    rsB.at[st, k - 1, half], {"band": zpeer(k)},
+                )
+                copy.start()
+                copies_b.append(copy)
+            S1[0, part] = SB[co, zi, part] + RA[st, zi, part]
         for copy in copies_b:
             copy.wait_recv()
         total = S1[0] + RB[st, 0] + RB[st, 1] + RB[st, 2]
@@ -275,28 +297,40 @@
                     part = out[j * 8 : j * 8 + 8, (2 + q) * 128 : (2 + q) * 128 + 128]
                     halo = jnp.where(slot == x2 * 8 + g, part, halo)
             OB[q, 16] = halo
-        copy_4 = send(OB.at[other], R4.at[st], ss4.at[st], rs4.at[st], {"sub": other})
-        copy_4.start()
-        copy_4.wait_recv()
-        AG[st, b] = OB[h] + R4[st]
-
-        gather = []
-        for k in range(1, 4):
+        parts = (pl.ds(0, 8), pl.ds(8, 9))
+        copies_4 = []
+        for half, part in enumerate(parts):
             copy = send(
-                AG.at[st, b], AG.at[st, b], ssG.at[st, k - 1], rsG.at[st, k - 1], {"band": zpeer(k)}
+                OB.at[other, part], R4.at[st, part], ss4.at[st, half], rs4.at[st, half], {"sub": other}
             )
             copy.start()
-            gather.append(copy)
-        forward = [send(AG.at[st, b], AG.at[st, b], ssH.at[st, 0], rsH.at[st, 0], {"band": mate})]
-        forward[0].start()
-        for k in range(1, 4):
-            gather[k - 1].wait_recv()
-            came = zpeer(4 - k)
-            copy = send(
-                AG.at[st, came], AG.at[st, came], ssH.at[st, k], rsH.at[st, k], {"band": mate}
-            )
+            copies_4.append(copy)
+
+        gather, forward = [], []
+
+        def pass_on(index, k, half):
+            block = AG.at[st, index, parts[half]]
+            copy = send(block, block, ssH.at[st, k, half], rsH.at[st, k, half], {"band": mate})
             copy.start()
             forward.append(copy)
+
+        for half, part in enumerate(parts):
+            copies_4[half].wait_recv()
+            AG[st, b, part] = OB[h, part] + R4[st, part]
+            block = AG.at[st, b, part]
+            for k in (2, 1, 3):
+                copy = send(
+                    block, block, ssG.at[st, k - 1, half], rsG.at[st, k - 1, half], {"band": zpeer(k)}
+                )
+                copy.start()
+                gather.append((k, half, copy))
+            pass_on(b, 0, half)
+        for half in range(2):
+            for k in (1, 3, 2):
+                for kk, hh, copy in gather:
+                    if (kk, hh) == (k, half):
+                        copy.wait_recv()
+                pass_on(zpeer(4 - k), k, half)
         for copy in forward:
             copy.wait_recv()
 
@@ -331,44 +365,38 @@
 
         def advance(o, carry):
             inv = INV[o, 0:1, :]
-
-            def scaled(tile):
-                return U[o, :, lanes(tile)] * HALF[:, lanes(tile)] * inv
-
-            squares = jnp.zeros((32, 128), F32)
-            before = jnp.zeros((32, 128), F32)
-            here = scaled(0)
-            turned = pltpu.roll(here, 64, 1)
+            for c in range(4):
+                rows = []
+                for tile in range(8 * c, 8 * c + 8):
+                    here = U[0, o, :, lanes(tile)] * HALF[:, lanes(tile)] * inv
+                    SC[tile] = here
+                    coarse = here.astype(jnp.bfloat16)
+                    fine = (here - coarse.astype(F32)).astype(jnp.bfloat16)
+                    rows.append(jnp.concatenate([coarse, fine], 1))
+                near = jnp.dot(jnp.concatenate(rows, 0), WS[...], preferred_element_type=F32)
+                MX[8 * c : 8 * c + 8] = near.reshape(8, 32, 256)
+            squares = zero8
             for tile in range(32):
-                if tile < 31:
-                    later = scaled(tile + 1)
-                    after = pltpu.roll(later, 64, 1)
-                else:
-                    later = here
-                    after = jnp.zeros((32, 128), F32)
-                next_y = pltpu.roll(jnp.where(first_y, turned, here), 127, 1)
-                prior_y = pltpu.roll(jnp.where(last_y, turned, here), 1, 1)
-                prior_z = jnp.where(
-                    row32 == 0, SH[0, o, tile : tile + 1, :], pltpu.roll(here, 1, 0)
-                )
-                next_z = jnp.where(
-                    row32 == 31, SH[1, o, tile : tile + 1, :], pltpu.roll(here, 31, 0)
-                )
-                around = turned + jnp.where(low32, before, after) + next_y + prior_y
-                around = around + prior_z + next_z
-                kept = 1.0 - 3.0 * TIME
-                value = (kept * here + 0.5 * TIME * around) * HALF[:, lanes(tile)]
-                U[o, :, lanes(tile)] = value
-                EDGES[st + 1, 0, o, tile : tile + 1, :] = value[31:32]
-                EDGES[st + 1, 1, o, tile : tile + 1, :] = value[0:1]
-                squares = squares + value * value
-                before, here, turned = turned, later, after
-            NBO[o] = squares[0:8] + squares[8:16] + squares[16:24] + squares[24:32]
-
-            @pl.when(st == STEPS - 1)
-            def _():
-                pltpu.make_async_copy(U.at[o], out_hbm.at[0, o], l_o.at[o]).start()
-
+                pieces = [SC[tile, 8 * i : 8 * i + 8] for i in range(4)]
+                up = [SH[0, o, tile : tile + 1, :]] + [pltpu.roll(v, 1, 0) for v in pieces]
+                down = [pltpu.roll(v, 7, 0) for v in pieces] + [SH[1, o, tile : tile + 1, :]]
+                for i in range(4):
+                    span = slice(8 * i, 8 * i + 8)
+                    before = MX[tile - 1, span, 128:] if tile > 0 else zero8
+                    after = MX[tile + 1, span, 128:] if tile < 31 else zero8
+                    around = MX[tile, span, :128] + jnp.where(low, before, after)
+                    around = around + jnp.where(top, up[i], up[i + 1])
+                    around = around + jnp.where(bottom, down[i + 1], down[i])
+                    kept = 1.0 - 3.0 * TIME
+                    value = kept * pieces[i] + 0.5 * TIME * around
+                    value = value * HALF[span, lanes(tile)]
+                    U[0, o, span, lanes(tile)] = value
+                    squares = squares + value * value
+                    if i == 3:
+                        EDGES[st + 1, 0, o, tile : tile + 1, :] = value[7:8]
+                    if i == 0:
+                        EDGES[st + 1, 1, o, tile : tile + 1, :] = value[0:1]
+            NBO[o] = squares
             return carry
 
         lax.fori_loop(0, 8, advance, 0)
@@ -377,62 +405,100 @@
             NB[st, o : o + 1, :] = jnp.sum(NBO[o], axis=0, keepdims=True)
         norm_copy = send(NB.at[st], NR.at[st], ssN.at[st], rsN.at[st], {"sub": other})
         norm_copy.start()
-        copy_a.wait_send()
-        for copy in copies_b + moment_copies + side_copies + gather + forward + [copy_4, edge_copy]:
+
+        @pl.when(st < STEPS - 1)
+        def _():
+            edges_of(st + 1).start()
+
+        for copy in copies_a + copies_b + moment_copies + side_copies + copies_4 + forward:
             copy.wait_send()
+        for _, _, copy in gather:
+            copy.wait_send()
+        edge_copy.wait_send()
         norm_copy.wait()
         norms = jnp.sum(NB[st] + NR[st], axis=1, keepdims=True)
         inv = jnp.broadcast_to(1.0 / jnp.sqrt(norms / CELLS + EPS), (8, 128))
         for o in range(8):
             INV[o] = jnp.broadcast_to(inv[o : o + 1], (8, 128))
         W8[...] = OCC8[...] * inv * inv
+
+        @pl.when(st < STEPS - 1)
+        def _():
+            density(st + 1, False)
+
         return carry
 
     lax.fori_loop(0, STEPS, step, 0)
+
+
+def scale_out(U, VB, INV, out_hbm, pot_hbm, buffer, sems):
+    copies = [pltpu.make_async_copy(VB, pot_hbm.at[0], sems.at[8])]
+    copies[0].start()
     for o in range(8):
-        inv_out[o : o + 1, :] = INV[o, 0:1, :]
-    last = pltpu.make_async_copy(VB, pot_hbm.at[0], l_o.at[8])
-    last.start()
-    for o in range(8):
-        pltpu.make_async_copy(U.at[o], out_hbm.at[0, o], l_o.at[o]).wait()
-    last.wait()
+        for tile in range(32):
+            lanes = pl.ds(tile * 128, 128)
+            buffer[o, :, lanes] = U[0, o, :, lanes] * INV[o, 0:1, :]
+        copy = pltpu.make_async_copy(buffer.at[o], out_hbm.at[0, o], sems.at[o])
+        copy.start()
+        copies.append(copy)
+    for copy in copies:
+        copy.wait()
 
 
 def body(orbitals, occupations, ext_potential, core_range):
-    consts = tables()
-    hbm = pl.BlockSpec(memory_space=pl.ANY)
+    operands = [orbitals, occupations, ext_potential, core_range]
+    operands += [jnp.asarray(c) for c in tables()]
+    hbm = pl.BlockSpec(memory_space=pltpu.HBM)
     smem = pl.BlockSpec(memory_space=pltpu.SMEM)
     vmem = pl.BlockSpec(memory_space=pltpu.VMEM)
     V = lambda *s: pltpu.VMEM(s, F32)
     D = lambda *s: pltpu.SemaphoreType.DMA(s)
-    out, pot, inv = pl.pallas_call(
+    state, pot, inv = pl.pallas_call(
         kernel,
         out_shape=(
-            jax.ShapeDtypeStruct(orbitals.shape, F32),
-            jax.ShapeDtypeStruct(ext_potential.shape, F32),
-            jax.ShapeDtypeStruct((8, 128), F32),
+            pltpu.VMEM(orbitals.shape, F32),
+            pltpu.VMEM(ext_potential.shape[1:], F32),
+            pltpu.VMEM((8, 8, 128), F32),
         ),
-        in_specs=[hbm, smem, hbm, smem] + [hbm] * 5,
-        out_specs=(hbm, hbm, vmem),
+        in_specs=[hbm, smem, hbm, smem] + [hbm] * 6,
+        out_specs=(vmem, vmem, vmem),
         scratch_shapes=[
-            V(8, 32, 4096), V(32, 4096), V(32, 4096), V(32, 4096),
+            V(32, 4096), V(32, 4096),
             V(128, 128), V(128, 128), V(128, 512), V(512, 512), V(11, 8, 128),
-            V(8, 128), V(8, 128), V(8, 8, 128),
+            pltpu.VMEM((256, 256), jnp.bfloat16),
+            V(8, 128), V(8, 128), V(32, 32, 128), V(32, 32, 256),
             V(2, 4, 16, 8, 128), V(3, 4, 16, 8, 128), V(4, 16, 8, 128), V(3, 3, 16, 8, 128),
             V(64, 8, 128), V(64, 8, 128), V(64, 8, 128),
             V(2, 8, 8, 128), V(3, 2, 8, 8, 128), V(3, 8, 8, 128), V(128, 512),
             V(2, 17, 8, 128), V(3, 17, 8, 128), V(3, 8, 17, 8, 128),
             V(4, 2, 8, 32, 128), V(3, 2, 8, 32, 128), V(2, 32, 128), V(2, 32, 128), V(2, 32, 128),
             V(2, 8, 32, 128), V(8, 8, 128), V(3, 8, 128), V(3, 8, 128),
-            D(8), D(6), D(3), D(3), D(3, 3), D(3, 3), D(3, 2), D(3, 2), D(3, 7), D(3, 7),
-            D(3), D(3), D(3, 3), D(3, 3), D(3, 4), D(3, 4), D(3), D(3), D(1), D(1), D(3), D(3), D(9),
+            D(8), D(7), D(3, 2), D(3, 2), D(3, 3, 2), D(3, 3, 2), D(3, 2), D(3, 2), D(3, 7), D(3, 7),
+            D(3, 2), D(3, 2), D(3, 3, 2), D(3, 3, 2), D(3, 4, 2), D(3, 4, 2),
+            D(3), D(3), D(1), D(1), D(3), D(3),
         ],
         compiler_params=pltpu.CompilerParams(
-            collective_id=0, has_side_effects=True, vmem_limit_bytes=60 * 1024 * 1024
+            collective_id=0, has_side_effects=True, vmem_limit_bytes=59 * 1024 * 1024
         ),
         name="steps",
-    )(orbitals, occupations, ext_potential, core_range, *[jnp.asarray(c) for c in consts])
-    return out * inv[:, 0][None, :, None, None], pot
+    )(
+        *[
+            v if i in (1, 3) else pltpu.with_memory_space_constraint(v, pltpu.HBM)
+            for i, v in enumerate(operands)
+        ]
+    )
+    return pl.pallas_call(
+        scale_out,
+        out_shape=(
+            jax.ShapeDtypeStruct(orbitals.shape, F32),
+            jax.ShapeDtypeStruct(ext_potential.shape, F32),
+        ),
+        in_specs=[vmem] * 3,
+        out_specs=(hbm, hbm),
+        scratch_shapes=[V(8, 32, 4096), D(9)],
+        compiler_params=pltpu.CompilerParams(vmem_limit_bytes=8 * 1024 * 1024),
+        name="scale_out",
+    )(state, pot, inv)
 
 
 def solution(mesh):

time: 120 us -> 97.8 us (0.81)
  Pallas kernels: 113 us -> 97.1 us
  other arithmetic: 4.82 us -> 0 us
  local copies, waits for them, and re-layouts: 1.58 us -> 0 us
    pallas_call x1 -> x2, Pallas kernels: 113 us -> 97.1 us  [the longest x1 94.8 us: body(): pl.pallas_call(kernel, out_shape=(pltpu.VMEM(orbitals.shape, F32), pltpu....]
    mul x1 -> x0, other arithmetic: 4.82 us -> none  [body(): return (out * inv[:, 0][None, :, None, None], pot)]
where the time goes in v2:
time: 97.8 us; the launch traced here: 97.7 us
  Pallas kernels  97.1 us (99%)
    pallas_call x1, Pallas kernels, body(): pl.pallas_call(kernel, out_shape=(pltpu.VMEM(orbitals.shape, F32), pltpu....  94.8 us
    pallas_call x1, Pallas kernels, body(): pl.pallas_call(scale_out, out_shape=(jax.ShapeDtypeStruct(orbitals.shape,...  2.25 us

profile of v2, /device:TPU:1, one launch (start us, length us, event | category | flops | bytes accessed | tf_op | source)
XLA Modules:
  0.0 97.7 jit_solution(16091721563022665072)
XLA Ops:
  0.6 94.8 %steps.1 = (f32[1,8,32,4096]{3,2,1,0:T(8,128)S(1)}, f32[32,4096]{1,0:T(8,128)S(1)}, f32[8,8,128]{2,1,0:T(8,128)S(1)}) custom-call(f32[1,8,32,4096]{3,2,1,0:T(8,128)} %orb_hbm.1, f32[1,8]{1,0:T(1,128)} %occ.1, f32[1,32,4096]{2,1,0:T(8,128)} %ext_hbm.1, s32[1,2]{1,0:T(1,128)} %core.1, f32[128,128]{1,0:T(8,128)} %constant.12.clone.wy_hbm, ...), custom_call_target="tpu_custom_call" | custom-call | tf_op jit(solution)/shard_map/steps/pallas_call | solution.py:456
  95.5 2.3 %scale_out.1 = (f32[1,8,32,4096]{3,2,1,0:T(8,128)}, f32[1,32,4096]{2,1,0:T(8,128)}) custom-call(f32[1,8,32,4096]{3,2,1,0:T(8,128)S(1)} %get-tuple-element.5.U, f32[32,4096]{1,0:T(8,128)S(1)} %get-tuple-element.6.VB, f32[8,8,128]{2,1,0:T(8,128)S(1)} %get-tuple-element.7.INV), custom_call_target="tpu_custom_call" | custom-call | tf_op jit(solution)/shard_map/scale_out/pallas_call | solution.py:490

commit v3 on v2

--- a/solution.py
+++ b/solution.py
@@ -39,9 +39,8 @@
     both = np.concatenate([full, full], 0)
     halo0 = np.tile(both[:, [63, 32]], (1, 16))
     halo1 = np.tile(both[:, [31, 0]], (1, 16))
-    w_i = np.concatenate(
-        [np.kron(np.eye(4), b) for b in (both[:, :32], both[:, 32:], halo0, halo1)], 1
-    )
+    w_i = [np.kron(np.eye(4), v) for v in (both[:, :32], halo0, both[:, 32:], halo1)]
+    w_i = np.stack([np.concatenate(w_i[:2], 1), np.concatenate(w_i[2:], 1)])
     lam = 2.0 - 2.0 * np.cos(2.0 * np.pi / EDGE * ids)
     a = lam[:, None] + lam[None, :] + SCREEN
     r = 1.0 / (1.0 + a / 2 + np.sqrt(a + a * a / 4))
@@ -68,7 +67,7 @@
     orb_hbm, occ, ext_hbm, core, wy_hbm, wh_hbm, wz_hbm, wi_hbm, modes_hbm, st_hbm,
     U, VB, INV,
     HALF, EXT, WY, WH, WZ, WI, MODES, WS, OCC8, W8, SC, MX,
-    SB, RA, S1, RB, S2, PP, PW, FS, FR, MV, QB, OB, R4, AG, EDGES, ER, EXTE, EXTR, HH, SH, NBO, NB, NR,
+    SB, RA, S1, RB, S2, S3, ST, PP, P2, PW, FR, MV, QB, OB, R4, AG, EDGES, ER, EXTE, EXTR, HH, SH, NBO, NB, NR,
     l_u, l_c, ssA, rsA, ssB, rsB, ssF, rsF, ssM, rsM, ss4, rs4, ssG, rsG, ssH, rsH, ssE, rsE,
     ssX, rsX, ssN, rsN,
 ):
@@ -111,7 +110,8 @@
         greet({"band": zpeer(k)})
     greet({"sub": other})
     for k in range(1, 8):
-        greet({"dom": (d + k) % 8})
+        for sub in (h, other):
+            greet({"dom": (d + k) % 8, "sub": sub})
 
     def send(src, dst, ss, rs, dev):
         return pltpu.make_async_remote_copy(
@@ -168,7 +168,7 @@
                         row = x2 * 64 + (2 * z + c) * 8
                         SB[c, z, 2 * g + x2] = out[row : row + 8]
             if g == 3 and first:
-                pl.semaphore_wait(barrier, 12)
+                pl.semaphore_wait(barrier, 19)
             if g % 4 == 3:
                 to_mate(st, g // 4).start()
 
@@ -219,9 +219,19 @@
             S1[0, part] = SB[co, zi, part] + RA[st, zi, part]
         for copy in copies_b:
             copy.wait_recv()
-        total = S1[0] + RB[st, 0] + RB[st, 1] + RB[st, 2]
-
-        out = dot(total.reshape(128, 128), WZ[...])
+        ST[...] = S1[0] + RB[st, 0] + RB[st, 1] + RB[st, 2]
+
+        dom_copies = []
+        for side, part, peer in ((0, pl.ds(12, 4), (d + 1) % 8), (1, pl.ds(0, 4), (d + 7) % 8)):
+            for i, sub in enumerate((h, other)):
+                copy = send(
+                    ST.at[part], FR.at[st, h, side], ssF.at[st, i, side], rsF.at[st, h, side],
+                    {"dom": peer, "sub": sub},
+                )
+                copy.start()
+                dom_copies.append(copy)
+
+        out = dot(ST[...].reshape(128, 128), WZ[...])
         scale = MODES[1 + h]
         r = MODES[0]
         for g in range(8):
@@ -234,77 +244,102 @@
         for i in range(64):
             p = p * r + jnp.where(low, S2[i], S2[63 - i])
             PP[i] = p
-        MV[st, d] = p
-        moment_copies = []
-        for k in range(1, 8):
-            copy = send(
-                MV.at[st, d], MV.at[st, d], ssM.at[st, k - 1], rsM.at[st, k - 1], {"dom": (d + k) % 8}
-            )
-            copy.start()
-            moment_copies.append(copy)
-
-        def response(x):
-            return jnp.where(low, PP[x] - S2[x], PP[63 - x])
-
-        side_copies = []
-        for side, base, peer in ((0, 48, (d + 1) % 8), (1, 0, (d + 7) % 8)):
-            for m in range(8):
-                even = response(base + 2 * m)
-                odd = response(base + 2 * m + 1)
-                even = even + pltpu.roll(even, 64, 1)
-                odd = odd + pltpu.roll(odd, 64, 1)
-                FS[side, m] = jnp.where(low, even, odd)
-            copy = send(
-                FS.at[side], FR.at[st, side], ssF.at[st, side], rsF.at[st, side], {"dom": peer}
-            )
-            copy.start()
-            side_copies.append(copy)
-
-        for copy in moment_copies:
-            copy.wait_recv()
-        for copy in side_copies:
-            copy.wait_recv()
-
-        incoming = zero8
-        for k in range(2, 10):
-            moved = jnp.where(low, MV[st, (d + 16 - k) % 8], MV[st, (d + k) % 8])
-            incoming = incoming + MODES[1 + k] * moved
-        near = jnp.where(low, MV[st, (d + 7) % 8], MV[st, (d + 1) % 8])
-        for i in range(64):
-            value = PP[i] + PW[i] * incoming
-            if i >= 16:
-                value = value + PW[i - 15] * near
-            PP[i] = value
-        for x in range(64):
-            value = response(x)
-            if x < 16:
-                part = FR[st, 0, x // 2]
-                value = value + jnp.where(low if x % 2 == 0 else ~low, part, 0.0)
-            if x >= 48:
-                part = FR[st, 1, (x - 48) // 2]
-                value = value + jnp.where(low if x % 2 == 0 else ~low, part, 0.0)
-            g, t, x2 = x // 8, (x % 8) // 2, x % 2
-            row = (2 * g + x2) * 8
+            if i == 47:
+                MV[st, h, d, 0] = p
+        MV[st, h, d, 1] = p
+        mine = MV.at[st, h, d]
+        for k in range(8):
+            for i, sub in enumerate((h, other)):
+                if k + i > 0:
+                    copy = send(
+                        mine, mine, ssM.at[st, i, k], rsM.at[st, h, k],
+                        {"dom": (d + k) % 8, "sub": sub},
+                    )
+                    copy.start()
+                    dom_copies.append(copy)
+
+        def place(x, value):
+            row = (2 * (x // 8) + x % 2) * 8
+            t = (x % 8) // 2
             QB[row : row + 8, t * 128 : t * 128 + 128] = value
 
-        out = dot(QB[...], WI[...])
-        for q in range(2):
+        def planes(q, put):
+            out = dot(QB[...], WI[q])
             halo = zero8
             for g in range(8):
                 for x2 in range(2):
                     j = 2 * g + x2
-                    OB[q, j] = out[j * 8 : j * 8 + 8, q * 128 : q * 128 + 128]
-                    part = out[j * 8 : j * 8 + 8, (2 + q) * 128 : (2 + q) * 128 + 128]
+                    put(j, out[j * 8 : j * 8 + 8, :128])
+                    part = out[j * 8 : j * 8 + 8, 128:]
                     halo = jnp.where(slot == x2 * 8 + g, part, halo)
-            OB[q, 16] = halo
+            put(16, halo)
+
+        for x in range(64):
+            place(x, jnp.where(low, PP[x] - S2[x], PP[63 - x]))
+
+        def to_other(j, value):
+            OB[j] = value
+
+        planes(other, to_other)
+        copy_4 = send(OB, R4.at[st], ss4.at[st], rs4.at[st], {"sub": other})
+        copy_4.start()
+
+        def arrived(sub, index, sems, where):
+            return send(where, where, sems.at[st, sub, index], sems.at[st, sub, index], {"sub": other})
+
+        for side in range(2):
+            for sub in range(2):
+                arrived(sub, side, rsF, FR.at[st, sub, side]).wait_recv()
+        out = dot(FR[st].reshape(128, 128), WZ[...])
+        for side in range(2):
+            for j in range(4):
+                for t in range(4):
+                    row = (side * 4 + j) * 8
+                    span = slice(t * 128, t * 128 + 128)
+                    value = out[row : row + 8, span] * MODES[1]
+                    value = value + out[row + 64 : row + 72, span] * MODES[2]
+                    S3[side * 16 + 8 * (j // 2) + 2 * t + j % 2] = value
+        p = zero8
+        for i in range(64):
+            p = p * r
+            if i < 16:
+                p = p + jnp.where(low, S3[i], S3[31 - i])
+            if i >= 48:
+                p = p + jnp.where(low, S3[i - 32], S3[63 - i])
+            P2[i] = PP[i] + p
+
+        for k in range(8):
+            for i, sub in enumerate((h, other)):
+                if k + i > 0:
+                    arrived(sub, k, rsM, MV.at[st, sub, (d + 8 - k) % 8]).wait_recv()
+
+        def moment(k, which):
+            left, right = (d + 16 - k) % 8, (d + k) % 8
+            return jnp.where(
+                low,
+                MV[st, 0, left, which] + MV[st, 1, left, which],
+                MV[st, 0, right, which] + MV[st, 1, right, which],
+            )
+
+        incoming = r * moment(1, 0)
+        for k in range(2, 10):
+            incoming = incoming + MODES[1 + k] * moment(k, 1)
+        for x in range(64):
+            source = S2[x]
+            if x < 16:
+                source = source + S3[x]
+            if x >= 48:
+                source = source + S3[x - 32]
+            forth = P2[x] + PW[x] * incoming
+            back = P2[63 - x] + PW[63 - x] * incoming
+            place(x, jnp.where(low, forth - source, back))
+        copy_4.wait_recv()
+
+        def to_band(j, value):
+            AG[st, b, j] = value + R4[st, j]
+
+        planes(h, to_band)
         parts = (pl.ds(0, 8), pl.ds(8, 9))
-        copies_4 = []
-        for half, part in enumerate(parts):
-            copy = send(
-                OB.at[other, part], R4.at[st, part], ss4.at[st, half], rs4.at[st, half], {"sub": other}
-            )
-            copy.start()
-            copies_4.append(copy)
 
         gather, forward = [], []
 
@@ -315,8 +350,6 @@
             forward.append(copy)
 
         for half, part in enumerate(parts):
-            copies_4[half].wait_recv()
-            AG[st, b, part] = OB[h, part] + R4[st, part]
             block = AG.at[st, b, part]
             for k in (2, 1, 3):
                 copy = send(
@@ -410,7 +443,7 @@
         def _():
             edges_of(st + 1).start()
 
-        for copy in copies_a + copies_b + moment_copies + side_copies + copies_4 + forward:
+        for copy in copies_a + copies_b + dom_copies + [copy_4] + forward:
             copy.wait_send()
         for _, _, copy in gather:
             copy.wait_send()
@@ -464,17 +497,17 @@
         out_specs=(vmem, vmem, vmem),
         scratch_shapes=[
             V(32, 4096), V(32, 4096),
-            V(128, 128), V(128, 128), V(128, 512), V(512, 512), V(11, 8, 128),
+            V(128, 128), V(128, 128), V(128, 512), V(2, 512, 256), V(11, 8, 128),
             pltpu.VMEM((256, 256), jnp.bfloat16),
             V(8, 128), V(8, 128), V(32, 32, 128), V(32, 32, 256),
             V(2, 4, 16, 8, 128), V(3, 4, 16, 8, 128), V(4, 16, 8, 128), V(3, 3, 16, 8, 128),
-            V(64, 8, 128), V(64, 8, 128), V(64, 8, 128),
-            V(2, 8, 8, 128), V(3, 2, 8, 8, 128), V(3, 8, 8, 128), V(128, 512),
-            V(2, 17, 8, 128), V(3, 17, 8, 128), V(3, 8, 17, 8, 128),
+            V(64, 8, 128), V(32, 8, 128), V(16, 8, 128), V(64, 8, 128), V(64, 8, 128), V(64, 8, 128),
+            V(3, 2, 2, 4, 8, 128), V(3, 2, 8, 2, 8, 128), V(128, 512),
+            V(17, 8, 128), V(3, 17, 8, 128), V(3, 8, 17, 8, 128),
             V(4, 2, 8, 32, 128), V(3, 2, 8, 32, 128), V(2, 32, 128), V(2, 32, 128), V(2, 32, 128),
             V(2, 8, 32, 128), V(8, 8, 128), V(3, 8, 128), V(3, 8, 128),
-            D(8), D(7), D(3, 2), D(3, 2), D(3, 3, 2), D(3, 3, 2), D(3, 2), D(3, 2), D(3, 7), D(3, 7),
-            D(3, 2), D(3, 2), D(3, 3, 2), D(3, 3, 2), D(3, 4, 2), D(3, 4, 2),
+            D(8), D(7), D(3, 2), D(3, 2), D(3, 3, 2), D(3, 3, 2), D(3, 2, 2), D(3, 2, 2), D(3, 2, 8), D(3, 2, 8),
+            D(3), D(3), D(3, 3, 2), D(3, 3, 2), D(3, 4, 2), D(3, 4, 2),
             D(3), D(3), D(1), D(1), D(3), D(3),
         ],
         compiler_params=pltpu.CompilerParams(

time: 97.8 us -> 90.6 us (0.926)
  Pallas kernels: 97.1 us -> 89.9 us
    pallas_call x1, Pallas kernels: 94.8 us -> 87.6 us  [body(): pl.pallas_call(kernel, out_shape=(pltpu.VMEM(orbitals.shape, F32), pltpu....]
where the time goes in v3:
time: 90.6 us; the launch traced here: 90.5 us
  Pallas kernels  89.9 us (99%)
    pallas_call x1, Pallas kernels, body(): pl.pallas_call(kernel, out_shape=(pltpu.VMEM(orbitals.shape, F32), pltpu....  87.6 us
    pallas_call x1, Pallas kernels, body(): pl.pallas_call(scale_out, out_shape=(jax.ShapeDtypeStruct(orbitals.shape,...  2.25 us

profile of v3, /device:TPU:1, one launch (start us, length us, event | category | flops | bytes accessed | tf_op | source)
XLA Modules:
  0.0 90.5 jit_solution(14297851590866102529)
XLA Ops:
  0.6 87.6 %steps.1 = (f32[1,8,32,4096]{3,2,1,0:T(8,128)S(1)}, f32[32,4096]{1,0:T(8,128)S(1)}, f32[8,8,128]{2,1,0:T(8,128)S(1)}) custom-call(f32[1,8,32,4096]{3,2,1,0:T(8,128)} %orb_hbm.1, f32[1,8]{1,0:T(1,128)} %occ.1, f32[1,32,4096]{2,1,0:T(8,128)} %ext_hbm.1, s32[1,2]{1,0:T(1,128)} %core.1, f32[128,128]{1,0:T(8,128)} %constant.12.clone.wy_hbm, ...), custom_call_target="tpu_custom_call" | custom-call | tf_op jit(solution)/shard_map/steps/pallas_call | solution.py:489
  88.2 2.3 %scale_out.1 = (f32[1,8,32,4096]{3,2,1,0:T(8,128)}, f32[1,32,4096]{2,1,0:T(8,128)}) custom-call(f32[1,8,32,4096]{3,2,1,0:T(8,128)S(1)} %get-tuple-element.5.U, f32[32,4096]{1,0:T(8,128)S(1)} %get-tuple-element.6.VB, f32[8,8,128]{2,1,0:T(8,128)S(1)} %get-tuple-element.7.INV), custom_call_target="tpu_custom_call" | custom-call | tf_op jit(solution)/shard_map/scale_out/pallas_call | solution.py:523

commit v4 on v3

--- a/solution.py
+++ b/solution.py
@@ -53,6 +53,7 @@
     modes = np.concatenate([modes, modes], 2).reshape(11, N_BAND, 8, 128).transpose(1, 0, 2, 3)
     swap = np.kron(1.0 - np.eye(2), np.eye(64))
     ring = np.roll(np.eye(64), 1, 0) + np.roll(np.eye(64), -1, 0)
+    ring = ring + (1.0 / (0.5 * TIME) - 6.0) * np.eye(64)
     stencil = np.concatenate([np.kron(np.eye(2), ring) + swap, swap], 1)
     stencil = np.concatenate([stencil, stencil], 0)
     out = [np.asarray(v, np.float32) for v in (w_y, w_h, w_z, w_i, modes)]
@@ -66,7 +67,7 @@
 def kernel(
     orb_hbm, occ, ext_hbm, core, wy_hbm, wh_hbm, wz_hbm, wi_hbm, modes_hbm, st_hbm,
     U, VB, INV,
-    HALF, EXT, WY, WH, WZ, WI, MODES, WS, OCC8, W8, SC, MX,
+    HALF, HT, EXT, WY, WH, WZ, WI, MODES, WS, OCC8, W8, SC, MX,
     SB, RA, S1, RB, S2, S3, ST, PP, P2, PW, FR, MV, QB, OB, R4, AG, EDGES, ER, EXTE, EXTR, HH, SH, NBO, NB, NR,
     l_u, l_c, ssA, rsA, ssB, rsB, ssF, rsF, ssM, rsM, ss4, rs4, ssG, rsG, ssH, rsH, ssE, rsE,
     ssX, rsX, ssN, rsN,
@@ -82,8 +83,16 @@
     def zpeer(k):
         return ((zi + k) % 4) * 2 + co
 
-    loads = [pltpu.make_async_copy(orb_hbm.at[0, o], U.at[0, o], l_u.at[o]) for o in range(8)]
-    loads += [
+    loads = [
+        pltpu.make_async_copy(
+            orb_hbm.at[0, o, :, pl.ds(2048 * half, 2048)],
+            U.at[0, o, :, pl.ds(2048 * half, 2048)],
+            l_u.at[half, o],
+        )
+        for half in range(2)
+        for o in range(8)
+    ]
+    consts = [
         pltpu.make_async_copy(src, dst, l_c.at[i])
         for i, (src, dst) in enumerate(
             (
@@ -97,7 +106,7 @@
             )
         )
     ]
-    for c in loads:
+    for c in consts[:1] + loads:
         c.start()
 
     barrier = pltpu.get_barrier_semaphore()
@@ -122,9 +131,6 @@
     low = lane < 64
     lane16 = lax.broadcasted_iota(jnp.int32, (16, 128), 1)
     lane32 = lax.broadcasted_iota(jnp.int32, (32, 128), 1)
-    row8 = lax.broadcasted_iota(jnp.int32, (8, 128), 0)
-    top = row8 == 0
-    bottom = row8 == 7
     slot = (lane % 32) // 2
     zero8 = jnp.zeros((8, 128), F32)
 
@@ -151,6 +157,9 @@
 
     def density(st, first):
         for g in range(8):
+            if first and g % 4 == 0:
+                for c in loads[2 * g : 2 * g + 8]:
+                    c.wait()
             tiles = []
             for t in range(4):
                 tile = 4 * g + t
@@ -172,10 +181,11 @@
             if g % 4 == 3:
                 to_mate(st, g // 4).start()
 
-    for c in loads[:9]:
-        c.wait()
+    consts[0].wait()
+    for c in consts[1:]:
+        c.start()
     density(0, True)
-    for c in loads[9:]:
+    for c in consts[1:]:
         c.wait()
 
     for tile in range(32):
@@ -347,7 +357,7 @@
             block = AG.at[st, index, parts[half]]
             copy = send(block, block, ssH.at[st, k, half], rsH.at[st, k, half], {"band": mate})
             copy.start()
-            forward.append(copy)
+            forward.append((half, copy))
 
         for half, part in enumerate(parts):
             block = AG.at[st, b, part]
@@ -364,10 +374,11 @@
                     if (kk, hh) == (k, half):
                         copy.wait_recv()
                 pass_on(zpeer(4 - k), k, half)
-        for copy in forward:
-            copy.wait_recv()
-
         for g in range(8):
+            if g % 4 == 0:
+                for half, copy in forward:
+                    if half == g // 4:
+                        copy.wait_recv()
             parts = [AG[st, :, 2 * g + x2].reshape(64, 128) for x2 in range(2)]
             cols = jnp.concatenate(parts, 0).T
             out = dot(cols, WY[...])
@@ -375,7 +386,9 @@
                 tile = 4 * g + t
                 value = out[t * 32 : t * 32 + 32]
                 VB[:, lanes(tile)] = value
-                HALF[:, lanes(tile)] = jnp.exp(-0.5 * TIME * (value + EXT[:, lanes(tile)]))
+                half = jnp.exp(-0.5 * TIME * (value + EXT[:, lanes(tile)]))
+                HALF[:, lanes(tile)] = half
+                HT[:, lanes(tile)] = 0.5 * TIME * half
 
         @pl.when(st == 0)
         def _():
@@ -402,7 +415,9 @@
                 rows = []
                 for tile in range(8 * c, 8 * c + 8):
                     here = U[0, o, :, lanes(tile)] * HALF[:, lanes(tile)] * inv
-                    SC[tile] = here
+                    SC[tile, 8:40] = here
+                    SC[tile, 7:8] = SH[0, o, tile : tile + 1, :]
+                    SC[tile, 40:41] = SH[1, o, tile : tile + 1, :]
                     coarse = here.astype(jnp.bfloat16)
                     fine = (here - coarse.astype(F32)).astype(jnp.bfloat16)
                     rows.append(jnp.concatenate([coarse, fine], 1))
@@ -410,19 +425,14 @@
                 MX[8 * c : 8 * c + 8] = near.reshape(8, 32, 256)
             squares = zero8
             for tile in range(32):
-                pieces = [SC[tile, 8 * i : 8 * i + 8] for i in range(4)]
-                up = [SH[0, o, tile : tile + 1, :]] + [pltpu.roll(v, 1, 0) for v in pieces]
-                down = [pltpu.roll(v, 7, 0) for v in pieces] + [SH[1, o, tile : tile + 1, :]]
                 for i in range(4):
                     span = slice(8 * i, 8 * i + 8)
                     before = MX[tile - 1, span, 128:] if tile > 0 else zero8
                     after = MX[tile + 1, span, 128:] if tile < 31 else zero8
                     around = MX[tile, span, :128] + jnp.where(low, before, after)
-                    around = around + jnp.where(top, up[i], up[i + 1])
-                    around = around + jnp.where(bottom, down[i + 1], down[i])
-                    kept = 1.0 - 3.0 * TIME
-                    value = kept * pieces[i] + 0.5 * TIME * around
-                    value = value * HALF[span, lanes(tile)]
+                    around = around + SC[tile, 7 + 8 * i : 15 + 8 * i]
+                    around = around + SC[tile, 9 + 8 * i : 17 + 8 * i]
+                    value = around * HT[span, lanes(tile)]
                     U[0, o, span, lanes(tile)] = value
                     squares = squares + value * value
                     if i == 3:
@@ -443,10 +453,10 @@
         def _():
             edges_of(st + 1).start()
 
-        for copy in copies_a + copies_b + dom_copies + [copy_4] + forward:
+        for copy in copies_a + copies_b + dom_copies + [copy_4]:
             copy.wait_send()
-        for _, _, copy in gather:
-            copy.wait_send()
+        for entry in gather + forward:
+            entry[-1].wait_send()
         edge_copy.wait_send()
         norm_copy.wait()
         norms = jnp.sum(NB[st] + NR[st], axis=1, keepdims=True)
@@ -496,17 +506,17 @@
         in_specs=[hbm, smem, hbm, smem] + [hbm] * 6,
         out_specs=(vmem, vmem, vmem),
         scratch_shapes=[
-            V(32, 4096), V(32, 4096),
+            V(32, 4096), V(32, 4096), V(32, 4096),
             V(128, 128), V(128, 128), V(128, 512), V(2, 512, 256), V(11, 8, 128),
             pltpu.VMEM((256, 256), jnp.bfloat16),
-            V(8, 128), V(8, 128), V(32, 32, 128), V(32, 32, 256),
+            V(8, 128), V(8, 128), V(32, 48, 128), V(32, 32, 256),
             V(2, 4, 16, 8, 128), V(3, 4, 16, 8, 128), V(4, 16, 8, 128), V(3, 3, 16, 8, 128),
             V(64, 8, 128), V(32, 8, 128), V(16, 8, 128), V(64, 8, 128), V(64, 8, 128), V(64, 8, 128),
             V(3, 2, 2, 4, 8, 128), V(3, 2, 8, 2, 8, 128), V(128, 512),
             V(17, 8, 128), V(3, 17, 8, 128), V(3, 8, 17, 8, 128),
             V(4, 2, 8, 32, 128), V(3, 2, 8, 32, 128), V(2, 32, 128), V(2, 32, 128), V(2, 32, 128),
             V(2, 8, 32, 128), V(8, 8, 128), V(3, 8, 128), V(3, 8, 128),
-            D(8), D(7), D(3, 2), D(3, 2), D(3, 3, 2), D(3, 3, 2), D(3, 2, 2), D(3, 2, 2), D(3, 2, 8), D(3, 2, 8),
+            D(2, 8), D(7), D(3, 2), D(3, 2), D(3, 3, 2), D(3, 3, 2), D(3, 2, 2), D(3, 2, 2), D(3, 2, 8), D(3, 2, 8),
             D(3), D(3), D(3, 3, 2), D(3, 3, 2), D(3, 4, 2), D(3, 4, 2),
             D(3), D(3), D(1), D(1), D(3), D(3),
         ],

time: 90.6 us -> 89.4 us (0.987)
  Pallas kernels: 89.9 us -> 88.6 us
    pallas_call x1, Pallas kernels: 87.6 us -> 86.3 us  [body(): pl.pallas_call(kernel, out_shape=(pltpu.VMEM(orbitals.shape, F32), pltpu....]
where the time goes in v4:
time: 89.4 us; the launch traced here: 89.2 us
  Pallas kernels  88.6 us (99%)
    pallas_call x1, Pallas kernels, body(): pl.pallas_call(kernel, out_shape=(pltpu.VMEM(orbitals.shape, F32), pltpu....  86.3 us
    pallas_call x1, Pallas kernels, body(): pl.pallas_call(scale_out, out_shape=(jax.ShapeDtypeStruct(orbitals.shape,...  2.25 us

profile of v4, /device:TPU:1, one launch (start us, length us, event | category | flops | bytes accessed | tf_op | source)
XLA Modules:
  0.0 89.2 jit_solution(13364827507621979765)
XLA Ops:
  0.6 86.3 %steps.1 = (f32[1,8,32,4096]{3,2,1,0:T(8,128)S(1)}, f32[32,4096]{1,0:T(8,128)S(1)}, f32[8,8,128]{2,1,0:T(8,128)S(1)}) custom-call(f32[1,8,32,4096]{3,2,1,0:T(8,128)} %orb_hbm.1, f32[1,8]{1,0:T(1,128)} %occ.1, f32[1,32,4096]{2,1,0:T(8,128)} %ext_hbm.1, s32[1,2]{1,0:T(1,128)} %core.1, f32[128,128]{1,0:T(8,128)} %constant.12.clone.wy_hbm, ...), custom_call_target="tpu_custom_call" | custom-call | tf_op jit(solution)/shard_map/steps/pallas_call | solution.py:499
  87.0 2.3 %scale_out.1 = (f32[1,8,32,4096]{3,2,1,0:T(8,128)}, f32[1,32,4096]{2,1,0:T(8,128)}) custom-call(f32[1,8,32,4096]{3,2,1,0:T(8,128)S(1)} %get-tuple-element.5.U, f32[32,4096]{1,0:T(8,128)S(1)} %get-tuple-element.6.VB, f32[8,8,128]{2,1,0:T(8,128)S(1)} %get-tuple-element.7.INV), custom_call_target="tpu_custom_call" | custom-call | tf_op jit(solution)/shard_map/scale_out/pallas_call | solution.py:533

commit v5 on v4

--- a/solution.py
+++ b/solution.py
@@ -28,6 +28,12 @@
 def cas(rows, cols, n):
     angle = 2.0 * np.pi / n * ((rows[:, None] * cols[None, :]) % n)
     return np.cos(angle) + np.sin(angle)
+
+
+def halves(v):
+    v = np.asarray(v, np.float32)
+    coarse = v.astype(jnp.bfloat16)
+    return np.stack([coarse, (v - coarse.astype(np.float32)).astype(jnp.bfloat16)])
 
 
 def tables():
@@ -56,12 +62,21 @@
     ring = ring + (1.0 / (0.5 * TIME) - 6.0) * np.eye(64)
     stencil = np.concatenate([np.kron(np.eye(2), ring) + swap, swap], 1)
     stencil = np.concatenate([stencil, stencil], 0)
-    out = [np.asarray(v, np.float32) for v in (w_y, w_h, w_z, w_i, modes)]
+    out = [np.asarray(v, np.float32) for v in (w_y, w_h)] + [halves(w_z), halves(w_i)]
+    out.append(np.asarray(modes, np.float32))
     return out + [np.asarray(stencil, jnp.bfloat16)]
 
 
 def dot(a, b, dims=((1,), (0,))):
     return lax.dot_general(a, b, (dims, ((), ())), precision=HIGH, preferred_element_type=F32)
+
+
+def dot_split(a, coarse_b, fine_b):
+    coarse = a.astype(jnp.bfloat16)
+    fine = (a - coarse.astype(F32)).astype(jnp.bfloat16)
+    out = jnp.dot(coarse, coarse_b, preferred_element_type=F32)
+    out = out + jnp.dot(fine, coarse_b, preferred_element_type=F32)
+    return out + jnp.dot(coarse, fine_b, preferred_element_type=F32)
 
 
 def kernel(
@@ -155,6 +170,13 @@
     def edges_of(st):
         return send(EDGES.at[st], ER.at[st], ssE.at[st], rsE.at[st], {"sub": other})
 
+    def weighted(tile, start):
+        acc = jnp.zeros((32, 128), F32)
+        for o in range(start, start + 4):
+            value = U[0, o, :, lanes(tile)]
+            acc = acc + value * value * W8[o : o + 1, :]
+        return acc
+
     def density(st, first):
         for g in range(8):
             if first and g % 4 == 0:
@@ -163,10 +185,8 @@
             tiles = []
             for t in range(4):
                 tile = 4 * g + t
-                acc = jnp.zeros((32, 128), F32)
-                for o in range(8):
-                    value = U[0, o, :, lanes(tile)]
-                    acc = acc + value * value * W8[o : o + 1, :]
+                acc = weighted(tile, 0) if first else SC[tile, 8:40]
+                acc = acc + weighted(tile, 4)
                 x = 2 * tile + lane32 // 64
                 tiles.append(jnp.where((x >= low_x) & (x < high_x), acc, 0.0))
             rho = jnp.concatenate(tiles, 0)
@@ -241,7 +261,7 @@
                 copy.start()
                 dom_copies.append(copy)
 
-        out = dot(ST[...].reshape(128, 128), WZ[...])
+        out = dot_split(ST[...].reshape(128, 128), WZ[0], WZ[1])
         scale = MODES[1 + h]
         r = MODES[0]
         for g in range(8):
@@ -274,7 +294,7 @@
             QB[row : row + 8, t * 128 : t * 128 + 128] = value
 
         def planes(q, put):
-            out = dot(QB[...], WI[q])
+            out = dot_split(QB[...], WI[0, q], WI[1, q])
             halo = zero8
             for g in range(8):
                 for x2 in range(2):
@@ -300,7 +320,7 @@
         for side in range(2):
             for sub in range(2):
                 arrived(sub, side, rsF, FR.at[st, sub, side]).wait_recv()
-        out = dot(FR[st].reshape(128, 128), WZ[...])
+        out = dot_split(FR[st].reshape(128, 128), WZ[0], WZ[1])
         for side in range(2):
             for j in range(4):
                 for t in range(4):
@@ -442,12 +462,14 @@
             NBO[o] = squares
             return carry
 
-        lax.fori_loop(0, 8, advance, 0)
-
-        for o in range(8):
-            NB[st, o : o + 1, :] = jnp.sum(NBO[o], axis=0, keepdims=True)
-        norm_copy = send(NB.at[st], NR.at[st], ssN.at[st], rsN.at[st], {"sub": other})
-        norm_copy.start()
+        norm_copies = []
+        for half in range(2):
+            lax.fori_loop(4 * half, 4 * half + 4, advance, 0)
+            for i in range(8):
+                NB[st, half, i : i + 1, :] = jnp.sum(NBO[4 * half + i % 4], axis=0, keepdims=True)
+            copy = send(NB.at[st, half], NR.at[st, half], ssN.at[st, half], rsN.at[st, half], {"sub": other})
+            copy.start()
+            norm_copies.append(copy)
 
         @pl.when(st < STEPS - 1)
         def _():
@@ -458,12 +480,24 @@
         for entry in gather + forward:
             entry[-1].wait_send()
         edge_copy.wait_send()
-        norm_copy.wait()
-        norms = jnp.sum(NB[st] + NR[st], axis=1, keepdims=True)
-        inv = jnp.broadcast_to(1.0 / jnp.sqrt(norms / CELLS + EPS), (8, 128))
-        for o in range(8):
-            INV[o] = jnp.broadcast_to(inv[o : o + 1], (8, 128))
-        W8[...] = OCC8[...] * inv * inv
+
+        def normalize(half):
+            norm_copies[half].wait()
+            norms = jnp.sum(NB[st, half] + NR[st, half], axis=1, keepdims=True)
+            inv = jnp.broadcast_to(1.0 / jnp.sqrt(norms / CELLS + EPS), (8, 128))[:4]
+            for i in range(4):
+                INV[4 * half + i] = jnp.broadcast_to(inv[i : i + 1], (8, 128))
+            span = slice(4 * half, 4 * half + 4)
+            W8[span, :] = OCC8[span, :] * inv * inv
+
+        normalize(0)
+
+        @pl.when(st < STEPS - 1)
+        def _():
+            for tile in range(32):
+                SC[tile, 8:40] = weighted(tile, 0)
+
+        normalize(1)
 
         @pl.when(st < STEPS - 1)
         def _():
@@ -507,7 +541,7 @@
         out_specs=(vmem, vmem, vmem),
         scratch_shapes=[
             V(32, 4096), V(32, 4096), V(32, 4096),
-            V(128, 128), V(128, 128), V(128, 512), V(2, 512, 256), V(11, 8, 128),
+            V(128, 128), V(128, 128), pltpu.VMEM((2, 128, 512), jnp.bfloat16), pltpu.VMEM((2, 2, 512, 256), jnp.bfloat16), V(11, 8, 128),
             pltpu.VMEM((256, 256), jnp.bfloat16),
             V(8, 128), V(8, 128), V(32, 48, 128), V(32, 32, 256),
             V(2, 4, 16, 8, 128), V(3, 4, 16, 8, 128), V(4, 16, 8, 128), V(3, 3, 16, 8, 128),
@@ -515,10 +549,10 @@
             V(3, 2, 2, 4, 8, 128), V(3, 2, 8, 2, 8, 128), V(128, 512),
             V(17, 8, 128), V(3, 17, 8, 128), V(3, 8, 17, 8, 128),
             V(4, 2, 8, 32, 128), V(3, 2, 8, 32, 128), V(2, 32, 128), V(2, 32, 128), V(2, 32, 128),
-            V(2, 8, 32, 128), V(8, 8, 128), V(3, 8, 128), V(3, 8, 128),
+            V(2, 8, 32, 128), V(8, 8, 128), V(3, 2, 8, 128), V(3, 2, 8, 128),
             D(2, 8), D(7), D(3, 2), D(3, 2), D(3, 3, 2), D(3, 3, 2), D(3, 2, 2), D(3, 2, 2), D(3, 2, 8), D(3, 2, 8),
             D(3), D(3), D(3, 3, 2), D(3, 3, 2), D(3, 4, 2), D(3, 4, 2),
-            D(3), D(3), D(1), D(1), D(3), D(3),
+            D(3), D(3), D(1), D(1), D(3, 2), D(3, 2),
         ],
         compiler_params=pltpu.CompilerParams(
             collective_id=0, has_side_effects=True, vmem_limit_bytes=59 * 1024 * 1024

time: 89.4 us -> 89.1 us (level)
  no operation moved by 1% of the time
where the time goes in v5:
time: 89.1 us; the launch traced here: 88.9 us
  Pallas kernels  88.3 us (99%)
    pallas_call x1, Pallas kernels, body(): pl.pallas_call(kernel, out_shape=(pltpu.VMEM(orbitals.shape, F32), pltpu....  86 us
    pallas_call x1, Pallas kernels, body(): pl.pallas_call(scale_out, out_shape=(jax.ShapeDtypeStruct(orbitals.shape,...  2.25 us

profile of v5, /device:TPU:1, one launch (start us, length us, event | category | flops | bytes accessed | tf_op | source)
XLA Modules:
  0.0 88.9 jit_solution(10180516848947950037)
XLA Ops:
  0.6 86.0 %steps.1 = (f32[1,8,32,4096]{3,2,1,0:T(8,128)S(1)}, f32[32,4096]{1,0:T(8,128)S(1)}, f32[8,8,128]{2,1,0:T(8,128)S(1)}) custom-call(f32[1,8,32,4096]{3,2,1,0:T(8,128)} %orb_hbm.1, f32[1,8]{1,0:T(1,128)} %occ.1, f32[1,32,4096]{2,1,0:T(8,128)} %ext_hbm.1, s32[1,2]{1,0:T(1,128)} %core.1, f32[128,128]{1,0:T(8,128)} %constant.12.clone.wy_hbm, ...), custom_call_target="tpu_custom_call" | custom-call | tf_op jit(solution)/shard_map/steps/pallas_call | solution.py:533
  86.7 2.3 %scale_out.1 = (f32[1,8,32,4096]{3,2,1,0:T(8,128)}, f32[1,32,4096]{2,1,0:T(8,128)}) custom-call(f32[1,8,32,4096]{3,2,1,0:T(8,128)S(1)} %get-tuple-element.5.U, f32[32,4096]{1,0:T(8,128)S(1)} %get-tuple-element.6.VB, f32[8,8,128]{2,1,0:T(8,128)S(1)} %get-tuple-element.7.INV), custom_call_target="tpu_custom_call" | custom-call | tf_op jit(solution)/shard_map/scale_out/pallas_call | solution.py:567
